TPU v7x, 32 devices: a whole 2x2x4 slice. The times are simulated.
32 devices in a mesh: dp: 2 (over x), sp: 4 (over z), cp: 4 (over y, core).
Axes of the slice: x: 2, y: 2, z: 4, core: 2. Of those that a mesh axis runs over, the one named last changes fastest.
Arguments:
- hidden: bfloat16 [8192, 3072], P(('dp', 'sp', 'cp')), parts along dimension 0
- g_kv: bfloat16 [3072], replicated
- w_k: bfloat16 [3072, 3072], replicated
- w_v: bfloat16 [3072, 3072], replicated
- g_attn: bfloat16 [2, 3072], replicated
- g_mlp: bfloat16 [2, 3072], replicated
- w_q: bfloat16 [2, 3072, 3072], replicated
- w_o: bfloat16 [2, 32, 96, 3072], replicated
- w_gate: bfloat16 [2, 3072, 8192], replicated
- w_up: bfloat16 [2, 3072, 8192], replicated
- w_down: bfloat16 [2, 8192, 3072], replicated
Outputs:
- output: bfloat16 [8192, 3072], P(('dp', 'sp', 'cp')), parts along dimension 0
There are 2 independent parts. A program takes and returns all parts, laid end to end along the dimension named above; an argument that names none is the same for every part.
All inputs are finite; a program needn't handle non-finite values.
Results may differ from a plain program's by a relative error of at most 0.0173681.
Values are sent between devices in bfloat16 or wider.
A program may use at most 1.75 GiB of HBM per device.

v0:
```python
import jax
import jax.numpy as jnp
from jax import lax
from jax.sharding import PartitionSpec as P

NEG_BIG = -1e30


def rms_norm(values, gain_vec):
    widened = values.astype(jnp.float32)
    inv_rms = lax.rsqrt(jnp.mean(widened * widened, axis=-1, keepdims=True) + 1e-6)
    return (widened * inv_rms * gain_vec.astype(jnp.float32)).astype(jnp.bfloat16)


def mlp_block(current, gain_vec, gate_w, up_w, down_w):
    normed = rms_norm(current, gain_vec)
    gate_out = jnp.dot(normed, gate_w, preferred_element_type=jnp.float32).astype(jnp.bfloat16)
    up_out = jnp.dot(normed, up_w, preferred_element_type=jnp.float32).astype(jnp.bfloat16)
    inner = (jax.nn.silu(gate_out.astype(jnp.float32)) * up_out.astype(jnp.float32)).astype(jnp.bfloat16)
    down_out = jnp.dot(inner, down_w, preferred_element_type=jnp.float32).astype(jnp.bfloat16)
    return (current.astype(jnp.float32) + down_out.astype(jnp.float32)).astype(jnp.bfloat16)


def causal_attention(query, keys_all, values_all, shard_index):
    rows = query.shape[0]
    score_scale = query.shape[-1] ** -0.5
    query_pos = shard_index * rows + jnp.arange(rows)

    def block_step(block_idx, carry):
        run_max, run_sum, accum = carry
        key_start = block_idx * rows
        key_block = lax.dynamic_slice_in_dim(keys_all, key_start, rows, axis=0)
        value_block = lax.dynamic_slice_in_dim(values_all, key_start, rows, axis=0)
        scores = jnp.einsum('trgd,sgd->trgs', query, key_block, preferred_element_type=jnp.float32) * score_scale
        allowed = (key_start + jnp.arange(rows))[None, :] <= query_pos[:, None]
        scores = jnp.where(allowed[:, None, None, :], scores, NEG_BIG)
        new_max = jnp.maximum(run_max, jnp.max(scores, axis=-1))
        probs = jnp.exp(scores - new_max[..., None])
        rescale = jnp.exp(run_max - new_max)
        run_sum = run_sum * rescale + jnp.sum(probs, axis=-1)
        accum = accum * rescale[..., None] + jnp.einsum('trgs,sgd->trgd', probs.astype(jnp.bfloat16), value_block, preferred_element_type=jnp.float32)
        return new_max, run_sum, accum

    init = (jnp.full(query.shape[:-1], NEG_BIG, jnp.float32), jnp.zeros(query.shape[:-1], jnp.float32), jnp.zeros(query.shape, jnp.float32))
    run_max, run_sum, accum = lax.fori_loop(0, shard_index + 1, block_step, init)
    return (accum / run_sum[..., None]).astype(jnp.bfloat16)


def solution(mesh):
    seq_axes = ('sp', 'cp')
    cp_size = mesh.shape['cp']
    row_spec = P(('dp', 'sp', 'cp'), None)

    def local(hidden, g_kv, w_k, w_v, g_attn, g_mlp, w_q, w_o, w_gate, w_up, w_down):
        rows, width = hidden.shape
        num_layers, n_heads, head_dim = w_o.shape[0], w_o.shape[1], w_o.shape[2]
        kv_heads = w_k.shape[1] // head_dim
        groups = n_heads // kv_heads
        shard_index = lax.axis_index('sp') * cp_size + lax.axis_index('cp')
        normed = rms_norm(hidden, g_kv)
        keys_local = jnp.dot(normed, w_k, preferred_element_type=jnp.float32).astype(jnp.bfloat16).reshape(rows, kv_heads, head_dim)
        values_local = jnp.dot(normed, w_v, preferred_element_type=jnp.float32).astype(jnp.bfloat16).reshape(rows, kv_heads, head_dim)
        keys_all = lax.all_gather(keys_local, seq_axes, axis=0, tiled=True)
        values_all = lax.all_gather(values_local, seq_axes, axis=0, tiled=True)
        current = hidden
        for layer in range(num_layers):
            query = jnp.dot(rms_norm(current, g_attn[layer]), w_q[layer], preferred_element_type=jnp.float32).astype(jnp.bfloat16)
            query = query.reshape(rows, groups, kv_heads, head_dim)
            mixed = causal_attention(query, keys_all, values_all, shard_index)
            wo_layer = w_o[layer].reshape(groups, kv_heads, head_dim, width)
            attn_out = jnp.einsum('trgd,rgdm->tm', mixed, wo_layer, preferred_element_type=jnp.float32).astype(jnp.bfloat16)
            current = (current.astype(jnp.float32) + attn_out.astype(jnp.float32)).astype(jnp.bfloat16)
            current = mlp_block(current, g_mlp[layer], w_gate[layer], w_up[layer], w_down[layer])
        return current

    return jax.shard_map(local, mesh=mesh, in_specs=(row_spec,) + (P(),) * 10, out_specs=row_spec, check_vma=False)
```

profile of v0, /device:TPU:29, one launch (start us, length us, event | category | flops | bytes accessed | tf_op | source)
XLA Modules:
  0.0 775.5 jit_solution(9357574980439164080)
XLA Ops:
  9.0 9.5 %convolution_convert_fusion.1 = bf16[256,3072]{1,0:T(8,128)(2,1)S(1)} fusion(bf16[3072,3072]{1,0:T(8,128)(2,1)} %param.17, bf16[256,3072]{1,0:T(8,128)(2,1)} %param.15, f32[3072]{0:T(1024)S(1)} %convert_element_type.134, f32[256]{0:T(256)S(1)} %add_rsqrt_fusion.3), kind=kOutput, calls=%fused_computation.131 | convolution fusion | flops 4835770368 | bytes 22033408 | tf_op jit(solution)/shard_map/dot_general | solution.py:61
  20.7 9.4 %convolution_convert_fusion = bf16[256,3072]{1,0:T(8,128)(2,1)S(1)} fusion(bf16[3072,3072]{1,0:T(8,128)(2,1)} %param.18, bf16[256,3072]{1,0:T(8,128)(2,1)S(1)} %copy-done, f32[3072]{0:T(1024)S(1)} %convert_element_type.134, f32[256]{0:T(256)S(1)} %add_rsqrt_fusion.3), kind=kOutput, calls=%fused_computation.130 | convolution fusion | flops 4835770368 | bytes 22033408 | tf_op jit(solution)/shard_map/dot_general | solution.py:62
  32.3 9.0 %fusion.146 = bf16[256,3072]{1,0:T(8,128)(2,1)S(1)} fusion(bf16[2,3072,3072]{2,1,0:T(8,128)(2,1)} %param.21, bf16[256,3072]{1,0:T(8,128)(2,1)S(1)} %copy-done, f32[3072]{0:T(1024)S(1)} %bitcast.301, f32[256]{0:T(256)S(1)} %add_rsqrt_fusion.3), kind=kOutput, calls=%fused_computation.128 | convolution fusion | flops 4835770368 | bytes 22033408 | tf_op jit(solution)/shard_map/dot_general | solution.py:67
  43.6 110.1 %all-gather.3.cloned.1.call-done = bf16[4096,32,96]{0,2,1:T(8,128)(2,1)} async-done(((bf16[256,32,96]{0,2,1:T(8,128)(2,1)}), bf16[4096,32,96]{0,2,1:T(8,128)(2,1)}) %all-gather.3.cloned.1.call-update) | async-done | bytes 25165840 | tf_op jit(solution)/shard_map/all_gather | solution.py:63
  153.7 134.5 %all-gather.5.cloned.1.call-done = bf16[4096,32,96]{0,2,1:T(8,128)(2,1)} async-done(((bf16[256,32,96]{0,2,1:T(8,128)(2,1)}), bf16[4096,32,96]{0,2,1:T(8,128)(2,1)}) %all-gather.5.cloned.1.call-update) | async-done | bytes 25165840 | tf_op jit(solution)/shard_map/all_gather | solution.py:64
  288.6 152.5 %while.30 = (s32[]{:T(128)}, f32[256,1,32]{0,2,1:T(8,128)S(1)}, f32[256,1,32]{0,2,1:T(8,128)S(1)}, f32[256,1,32,96]{0,3,2,1:T(8,128)S(1)}, s32[]{:T(128)}, /*ind...) while((s32[]{:T(128)}, f32[256,1,32]{0,2,1:T(8,128)S(1)}, ...), condition=%wide.region_4.0_spmd.clone, body=%wide.region_1.4_spmd.clone.sunk | while | flops 830038528 | bytes 36966584 | solution.py:45
  292.2 4.0 bitcast_add_fusion.9
  301.8 4.0 bitcast_add_fusion.9
  311.3 4.0 bitcast_add_fusion.9
  320.8 4.0 bitcast_add_fusion.9
  330.4 4.0 bitcast_add_fusion.9
  339.9 4.0 bitcast_add_fusion.9
  349.4 4.0 bitcast_add_fusion.9
  359.0 4.0 bitcast_add_fusion.9
  368.5 4.0 bitcast_add_fusion.9
  378.0 4.0 bitcast_add_fusion.9
  387.6 4.0 bitcast_add_fusion.9
  397.1 4.0 bitcast_add_fusion.9
  406.6 4.0 bitcast_add_fusion.9
  416.2 4.0 bitcast_add_fusion.9
  425.7 4.0 bitcast_add_fusion.9
  435.2 4.0 bitcast_add_fusion.9
  441.1 10.4 %fusion.195 = (f32[256]{0:T(256)S(1)}, bf16[256,3072]{1,0:T(8,128)(2,1)}) fusion(bf16[2,32,96,3072]{3,2,1,0:T(8,128)(2,1)} %param.22, f32[256,1,32,96]{0,3,2,1:T(8,128)S(1)} %get-tuple-element.103, f32[256,32]{0,1:T(8,128)S(1)} %bitcast.295, bf16[256,3072]{1,0:T(8,128)(2,1)} %param.15), kind=kOutput, calls=%fused_computation.143 | convolution fusion | flops 4839702528 | bytes 25199616 | tf_op jit(solution)/shard_map/trgd,rgdm->tm/dot_general | solution.py:71
  451.6 23.1 %fusion.76 = bf16[256,8192]{1,0:T(8,128)(2,1)} fusion(bf16[2,3072,8192]{2,1,0:T(8,128)(2,1)} %param.23, bf16[256,3072]{1,0:T(8,128)(2,1)} %get-tuple-element.222, f32[3072]{0:T(1024)S(1)} %bitcast.299, f32[256]{0:T(256)S(1)} %add_rsqrt_fusion.2), kind=kOutput, calls=%fused_computation.90 | convolution fusion | flops 12890144768 | bytes 56112128 | tf_op jit(solution)/shard_map/dot_general | solution.py:17
  474.7 22.8 %fusion.103.clone.9.clone.5 = bf16[256,8192]{1,0:T(8,128)(2,1)} fusion(bf16[2,3072,8192]{2,1,0:T(8,128)(2,1)} %param.24, bf16[256,8192]{1,0:T(8,128)(2,1)} %fusion.76, bf16[256,3072]{1,0:T(8,128)(2,1)S(1)} %copy-done.6, f32[3072]{0:T(1024)S(1)} %bitcast.300, f32[256]{0:T(256)S(1)} %add_rsqrt_fusion.2), kind=kOutput, calls=%fused_computation.99.clone.clone.clone.clone.clone.clone.clone.clone.clone.clone... | convolution fusion | flops 12906921984 | bytes 60306432 | tf_op jit(solution)/shard_map/dot_general | solution.py:18
  497.5 22.4 %fusion.198 = (f32[256]{0:T(256)S(1)}, bf16[256,3072]{1,0:T(8,128)(2,1)S(1)}) fusion(bf16[2,8192,3072]{2,1,0:T(8,128)(2,1)} %param.25, bf16[256,3072]{1,0:T(8,128)(2,1)} %get-tuple-element.222, bf16[256,8192]{1,0:T(8,128)(2,1)} %fusion.103.clone.9.clone.5), kind=kOutput, calls=%fused_computation.146 | convolution fusion | flops 12891193344 | bytes 57672704 | tf_op jit(solution)/shard_map/dot_general | solution.py:20
  519.9 9.6 %fusion.149 = bf16[256,3072]{1,0:T(8,128)(2,1)S(1)} fusion(bf16[2,3072,3072]{2,1,0:T(8,128)(2,1)} %param.21, bf16[256,3072]{1,0:T(8,128)(2,1)S(1)} %get-tuple-element.224, f32[3072]{0:T(1024)S(1)} %bitcast.298, f32[256]{0:T(256)S(1)} %add_rsqrt_fusion.1), kind=kOutput, calls=%fused_computation.129 | convolution fusion | flops 4835770368 | bytes 22033408 | tf_op jit(solution)/shard_map/dot_general | solution.py:67
  531.4 152.5 %while.31 = (s32[]{:T(128)}, f32[256,1,32]{0,2,1:T(8,128)S(1)}, f32[256,1,32]{0,2,1:T(8,128)S(1)}, f32[256,1,32,96]{0,3,2,1:T(8,128)S(1)}, s32[]{:T(128)}, /*ind...) while((s32[]{:T(128)}, f32[256,1,32]{0,2,1:T(8,128)S(1)}, ...), condition=%wide.region_10.11_spmd.clone, body=%wide.region_7.0_spmd.clone.sunk | while | flops 830038528 | bytes 36966584 | solution.py:45
  535.1 4.0 bitcast_add_fusion.11
  544.6 4.0 bitcast_add_fusion.11
  554.1 4.0 bitcast_add_fusion.11
  563.7 4.0 bitcast_add_fusion.11
  573.2 4.0 bitcast_add_fusion.11
  582.7 4.0 bitcast_add_fusion.11
  592.3 4.0 bitcast_add_fusion.11
  601.8 4.0 bitcast_add_fusion.11
  611.3 4.0 bitcast_add_fusion.11
  620.9 4.0 bitcast_add_fusion.11
  630.4 4.0 bitcast_add_fusion.11
  639.9 4.0 bitcast_add_fusion.11
  649.5 4.0 bitcast_add_fusion.11
  659.0 4.0 bitcast_add_fusion.11
  668.5 4.0 bitcast_add_fusion.11
  678.1 4.0 bitcast_add_fusion.11
  684.0 10.3 %fusion.201 = (f32[256]{0:T(256)S(1)}, bf16[256,3072]{1,0:T(8,128)(2,1)}) fusion(bf16[2,32,96,3072]{3,2,1,0:T(8,128)(2,1)} %param.22, f32[256,1,32,96]{0,3,2,1:T(8,128)S(1)} %get-tuple-element.105, f32[256,32]{0,1:T(8,128)S(1)} %bitcast.294, bf16[256,3072]{1,0:T(8,128)(2,1)} %copy-done.5), kind=kOutput, calls=%fused_computation.149 | convolution fusion | flops 4839702528 | bytes 25199616 | tf_op jit(solution)/shard_map/trgd,rgdm->tm/dot_general | solution.py:71
  694.3 28.3 %fusion.88 = bf16[256,8192]{1,0:T(8,128)(2,1)} fusion(bf16[2,3072,8192]{2,1,0:T(8,128)(2,1)} %param.23, bf16[256,3072]{1,0:T(8,128)(2,1)} %get-tuple-element.226, f32[3072]{0:T(1024)S(1)} %bitcast.296, f32[256]{0:T(256)S(1)} %add_rsqrt_fusion), kind=kOutput, calls=%fused_computation.94 | convolution fusion | flops 12890144768 | bytes 56112128 | tf_op jit(solution)/shard_map/dot_general | solution.py:17
  722.5 22.8 %fusion.100.clone.13 = bf16[256,8192]{1,0:T(8,128)(2,1)} fusion(bf16[2,3072,8192]{2,1,0:T(8,128)(2,1)} %param.24, bf16[256,8192]{1,0:T(8,128)(2,1)} %fusion.88, bf16[256,3072]{1,0:T(8,128)(2,1)S(1)} %copy-done.7, f32[3072]{0:T(1024)S(1)} %bitcast.297, f32[256]{0:T(256)S(1)} %add_rsqrt_fusion), kind=kOutput, calls=%fused_computation.98.clone.clone.clone.clone.clone.clone.clone.clone.clone.clone... | convolution fusion | flops 12906921984 | bytes 60306432 | tf_op jit(solution)/shard_map/dot_general | solution.py:18
  745.3 23.1 %fusion.185 = bf16[256,3072]{1,0:T(8,128)(2,1)} fusion(bf16[2,8192,3072]{2,1,0:T(8,128)(2,1)} %param.25, bf16[256,3072]{1,0:T(8,128)(2,1)S(1)} %copy-done.7, bf16[256,8192]{1,0:T(8,128)(2,1)} %fusion.100.clone.13), kind=kOutput, calls=%fused_computation.137 | convolution fusion | flops 12888834048 | bytes 57671680 | tf_op jit(solution)/shard_map/dot_general | solution.py:20
  (262 shorter events, 186.8 us)
Async XLA Ops:
  6.5 147.2 %all-gather.3.cloned.1.call-start = ((), (), s32[]{:S(2)}) async-start(), calls=%async_computation | async-start | bytes 26738688 | tf_op jit(solution)/shard_map/all_gather | solution.py:63
  18.5 2.2 copy-start
  20.1 268.1 %all-gather.5.cloned.1.call-start = ((), (), s32[]{:S(2)}) async-start(), calls=%async_computation.1 | async-start | bytes 26738688 | tf_op jit(solution)/shard_map/all_gather | solution.py:64
  30.1 1.6 copy-start.1
  41.4 1.6 copy-start.2
  451.6 23.1 %copy-start.6 = (bf16[256,3072]{1,0:T(8,128)(2,1)S(1)}, bf16[256,3072]{1,0:T(8,128)(2,1)}, u32[]{:S(2)}) copy-start(bf16[256,3072]{1,0:T(8,128)(2,1)} %get-tuple-element.222) | copy-start | bytes 4718596
  497.5 22.4 %copy-start.4 = (f32[1,3072]{1,0:T(1,128)S(1)}, f32[1,3072]{1,0:T(1,128)}, u32[]{:S(2)}) copy-start(f32[1,3072]{1,0:T(1,128)} %get-tuple-element.219) | copy-start | bytes 36868
  519.8 9.6 %copy-start.5 = (bf16[256,3072]{1,0:T(8,128)(2,1)}, bf16[256,3072]{1,0:T(8,128)(2,1)S(1)}, u32[]{:S(2)}) copy-start(bf16[256,3072]{1,0:T(8,128)(2,1)S(1)} %get-tuple-element.224) | copy-start | bytes 4718596
  683.9 10.3 %copy-start.3 = (f32[1,3072]{1,0:T(1,128)S(1)}, f32[1,3072]{1,0:T(1,128)}, u32[]{:S(2)}) copy-start(f32[1,3072]{1,0:T(1,128)} %get-tuple-element.217) | copy-start | bytes 36868
  694.2 28.3 %copy-start.7 = (bf16[256,3072]{1,0:T(8,128)(2,1)S(1)}, bf16[256,3072]{1,0:T(8,128)(2,1)}, u32[]{:S(2)}) copy-start(bf16[256,3072]{1,0:T(8,128)(2,1)} %get-tuple-element.226) | copy-start | bytes 4718596
Sparse Core Ops, SparseCore 0:
  20.3 133.3 all-gather.2
  155.2 132.9 all-gather.4
where the time goes:
time: 779 us; the launch traced here: 776 us
  matrix products  438 us (56%)
  waiting for transfers between devices  245 us (31%)
  other arithmetic  68.3 us (9%)
  between operations  13.9 us (2%)
    all_gather x1, waiting for transfers between devices, local(): values_all = lax.all_gather(values_local, seq_axes, axis=0, tiled=True)  135 us
    dot_general x32, matrix products, block_step(): jnp.einsum('trgs,sgd->trgd', probs.astype(jnp.bfloat16), value_block, pre...  127 us
    dot_general x32, matrix products, block_step(): jnp.einsum('trgd,sgd->trgs', query, key_block, preferred_element_type=jnp...  111 us
    all_gather x1, waiting for transfers between devices, local(): keys_all = lax.all_gather(keys_local, seq_axes, axis=0, tiled=True)  110 us
    reduce_sum x32, other arithmetic, block_step(): run_sum = run_sum * rescale + jnp.sum(probs, axis=-1)  59.7 us
    dot_general x2, matrix products, mlp_block(): jnp.dot(normed, gate_w, preferred_element_type=jnp.float32)  51.4 us
    dot_general x2, matrix products, mlp_block(): jnp.dot(normed, up_w, preferred_element_type=jnp.float32)  45.6 us
    dot_general x2, matrix products, mlp_block(): jnp.dot(inner, down_w, preferred_element_type=jnp.float32)  45.4 us
  transfers between devices with their start and end apart: 2, of which 2 were waited for; matrix products, arithmetic and copies ran while one was open for 3% of the time, Pallas kernels for 0%

commit v1 on v0

v1 whole, which is shorter than its diff:
```python
import functools

import jax
import jax.numpy as jnp
from jax import lax
from jax.experimental import pallas as pl
from jax.experimental.pallas import tpu as pltpu
from jax.sharding import PartitionSpec as P

F32 = jnp.float32
BF16 = jnp.bfloat16
NEG_BIG = -1e30
LOOKAHEAD = 4
COLS = 512
DOWN_COLS = 256
KV_CHUNKS = 4
LOG2E = 1.4426950408889634


def rms_norm(values, gain_vec):
    widened = values.astype(F32)
    inv_rms = lax.rsqrt(jnp.mean(widened * widened, axis=-1, keepdims=True) + 1e-6)
    return (widened * inv_rms * gain_vec.astype(F32)).astype(BF16)


def kv_kernel(core_ref, x_ref, wk_ref, wv_ref, *refs):
    k_ref, v_ref = refs[-2:]
    x = x_ref[...]
    shape = k_ref.shape
    k = jnp.dot(x, wk_ref[...], preferred_element_type=F32).astype(BF16)
    k_ref[...] = k.reshape(shape)
    v = jnp.dot(x, wv_ref[...], preferred_element_type=F32).astype(BF16)
    v_ref[...] = v.reshape(shape)


def kv_project(core, x, w_k, w_v, chunk, devices, prior):
    rows, width = x.shape
    half = w_k.shape[1] // 2
    part = rows // devices
    steps = half // COLS
    out_spec = pl.BlockSpec((devices, 1, part, COLS), lambda n, c: (0, chunk, 0, n))
    w_spec = pl.BlockSpec((width, COLS), lambda n, c: (0, c[0] * steps + n))
    full = jax.ShapeDtypeStruct((devices, KV_CHUNKS, part, half), BF16)
    in_specs = [pl.BlockSpec((rows, width), lambda n, c: (0, 0)), w_spec, w_spec]
    args = [core, x, w_k, w_v]
    aliases = {}
    if prior is not None:
        in_specs += [pl.BlockSpec(memory_space=pl.ANY)] * 2
        args += list(prior)
        aliases = {4: 0, 5: 1}
    return pl.pallas_call(
        kv_kernel,
        grid_spec=pltpu.PrefetchScalarGridSpec(
            num_scalar_prefetch=1, grid=(steps,), in_specs=in_specs, out_specs=[out_spec, out_spec]
        ),
        out_shape=[full, full],
        input_output_aliases=aliases,
        cost_estimate=pl.CostEstimate(
            flops=4 * rows * width * half, bytes_accessed=2 * (rows * width + 2 * width * half + 2 * rows * half), transcendentals=0
        ),
        name="kv_project",
    )(*args)


def attention_kernel(scale, info_ref, qa_ref, qb_ref, k_ref, v_ref, oa_ref, ob_ref, q_scr, m_scr, l_scr, acc_scr):
    rows = qa_ref.shape[0]
    span = 2 * rows
    full_blocks = info_ref[1]
    a_odd = info_ref[2]
    lane = lax.broadcasted_iota(jnp.int32, (rows, 256), 1)
    window_out = []
    for window in range(2):
        offset = 128 * window
        bounds = ((0, 96), (96, 192)) if window == 0 else ((64, 160), (160, 256))
        for head in range(2):
            lo, hi = bounds[head]
            keep = (lane >= lo) & (lane < hi)
            for part in range(2):
                q_src = qa_ref if part == 0 else qb_ref
                q_win = q_src[:, offset:offset + 256]
                q_scr[2 * head + part] = jnp.where(keep, q_win, jnp.zeros_like(q_win))
        m_scr[...] = jnp.full(m_scr.shape, NEG_BIG, F32)
        l_scr[...] = jnp.zeros(l_scr.shape, F32)
        acc_scr[...] = jnp.zeros(acc_scr.shape, F32)

        def step(block, masked, offset=offset):
            start = pl.multiple_of(block * span, span)
            k_win = k_ref[pl.ds(start, span), offset:offset + 256]
            v_win = v_ref[pl.ds(start, span), offset:offset + 256]
            for chain in range(4):
                s = lax.dot_general(q_scr[chain], k_win, (((1,), (1,)), ((), ())), preferred_element_type=F32)
                s = s * scale
                if masked:
                    odd = a_odd if chain % 2 == 0 else 1 - a_odd
                    row = lax.broadcasted_iota(jnp.int32, s.shape, 0) + odd * rows
                    col = lax.broadcasted_iota(jnp.int32, s.shape, 1)
                    s = jnp.where(col <= row, s, NEG_BIG)
                m_old = m_scr[chain]
                m_new = jnp.maximum(m_old, jnp.max(s, axis=1, keepdims=True))
                p = jnp.exp2(s - m_new[:, :1])
                alpha = jnp.exp2(m_old - m_new)
                part_sum = p[:, 0:128]
                for t in range(1, span // 128):
                    part_sum = part_sum + p[:, 128 * t:128 * t + 128]
                l_scr[chain] = l_scr[chain] * alpha + part_sum
                m_scr[chain] = m_new
                pv = jnp.dot(p.astype(BF16), v_win, preferred_element_type=F32)
                acc_scr[chain] = acc_scr[chain] * alpha[:, :1] + pv

        def body(block, carry):
            step(block, False)
            return carry

        lax.fori_loop(0, full_blocks, body, 0)
        step(full_blocks, True)
        outs = []
        for chain in range(4):
            total = jnp.sum(l_scr[chain], axis=1, keepdims=True)
            outs.append(acc_scr[chain] / total)
        split = bounds[0][1]
        window_out.append([
            jnp.where(lane < split, outs[part], outs[2 + part]).astype(BF16) for part in range(2)
        ])
        if window == 0:
            for part, o_ref in ((0, oa_ref), (1, ob_ref)):
                o_ref[:, 0:256] = window_out[0][part]
        else:
            for part, o_ref in ((0, oa_ref), (1, ob_ref)):
                second = window_out[1][part]
                middle = o_ref[:, 128:256]
                o_ref[:, 128:256] = jnp.where(lane[:, :128] < 64, middle, second[:, 0:128])
                o_ref[:, 256:384] = second[:, 128:256]


def attention(info, q_own, q_other, keys, values, head_dim):
    rows = q_own.shape[0]
    length, half = keys.shape
    group = 4 * head_dim
    groups = half // group
    q_own_spec = pl.BlockSpec((rows, group), lambda g, i: (0, i[0] * groups + g))
    col_spec = pl.BlockSpec((rows, group), lambda g, i: (0, g))
    kv_spec = pl.BlockSpec((length, group), lambda g, i: (0, g))
    out = jax.ShapeDtypeStruct((rows, half), BF16)
    scale = head_dim ** -0.5 * LOG2E
    return pl.pallas_call(
        functools.partial(attention_kernel, scale),
        grid_spec=pltpu.PrefetchScalarGridSpec(
            num_scalar_prefetch=1,
            grid=(groups,),
            in_specs=[q_own_spec, col_spec, kv_spec, kv_spec],
            out_specs=[col_spec, col_spec],
            scratch_shapes=[
                pltpu.VMEM((4, rows, 256), BF16),
                pltpu.VMEM((4, rows, 128), F32),
                pltpu.VMEM((4, rows, 128), F32),
                pltpu.VMEM((4, rows, 256), F32),
            ],
        ),
        out_shape=[out, out],
        cost_estimate=pl.CostEstimate(
            flops=8 * rows * length * half, bytes_accessed=4 * length * half, transcendentals=2 * rows * length * 16
        ),
        name="attention",
    )(info, q_own, q_other, keys, values)


def norm_into(dst_ref, src_ref, gain_ref):
    rows = src_ref.shape[0]
    gain = gain_ref[...].astype(F32)

    def body(i, carry):
        sl = pl.ds(pl.multiple_of(i * 32, 32), 32)
        wide = src_ref[sl, :].astype(F32)
        inv = lax.rsqrt(jnp.mean(wide * wide, axis=-1, keepdims=True) + 1e-6)
        dst_ref[sl, :] = (wide * inv * gain).astype(BF16)
        return carry

    lax.fori_loop(0, rows // 32, body, 0)


def query_kernel(layer, x_ref, gain_ref, wq_ref, q_ref, normed, ring, sems):
    width = x_ref.shape[1]
    tiles = q_ref.shape[1] // COLS

    def copy(t):
        return pltpu.make_async_copy(
            wq_ref.at[layer, :, pl.ds(pl.multiple_of(t * COLS, COLS), COLS)], ring.at[lax.rem(t, LOOKAHEAD)], sems.at[lax.rem(t, LOOKAHEAD)]
        )

    for t in range(LOOKAHEAD):
        copy(t).start()
    norm_into(normed, x_ref, gain_ref)

    def body(t, carry):
        copy(t).wait()
        out = jnp.dot(normed[...], ring[lax.rem(t, LOOKAHEAD)], preferred_element_type=F32)
        q_ref[:, pl.ds(pl.multiple_of(t * COLS, COLS), COLS)] = out.astype(BF16)

        @pl.when(t + LOOKAHEAD < tiles)
        def _():
            copy(t + LOOKAHEAD).start()

        return carry

    lax.fori_loop(0, tiles, body, 0)


def query_project(x, gain, w_q, layer):
    rows, width = x.shape
    vmem = pl.BlockSpec(memory_space=pltpu.VMEM)
    return pl.pallas_call(
        functools.partial(query_kernel, layer),
        in_specs=[vmem, vmem, pl.BlockSpec(memory_space=pl.ANY)],
        out_specs=vmem,
        out_shape=jax.ShapeDtypeStruct((rows, w_q.shape[2]), BF16),
        scratch_shapes=[
            pltpu.VMEM((rows, width), BF16),
            pltpu.VMEM((LOOKAHEAD, width, COLS), BF16),
            pltpu.SemaphoreType.DMA((LOOKAHEAD,)),
        ],
        cost_estimate=pl.CostEstimate(flops=2 * rows * width * width, bytes_accessed=2 * width * width, transcendentals=0),
        name="query_project",
    )(x, gain, w_q)


def layer_kernel(
    layer, has_next, core_ref, oa_ref, ob_ref, cur_ref, g_mlp_ref, g_next_ref, wo_ref, wg_ref, wu_ref, wd_ref, wq_ref,
    *refs,
):
    if has_next:
        out_ref, q_ref, mixed, normed, inner, ring, ring_down, sems = refs
    else:
        out_ref, mixed, normed, inner, ring, ring_down, sems = refs
        q_ref = None
    rows, width = cur_ref.shape
    hidden = wg_ref.shape[2]
    n_out = width // COLS
    n_up = hidden // COLS
    n_down = width // DOWN_COLS
    first_up = n_out
    first_down = n_out + 2 * n_up
    first_q = first_down + n_down
    total = first_q + (n_out if has_next else 0)

    def cols(i, size):
        return pl.ds(pl.multiple_of(i * size, size), size)

    def start(t):
        slot = lax.rem(t, LOOKAHEAD)

        def to_ring(src):
            pltpu.make_async_copy(src, ring.at[slot], sems.at[slot]).start()

        @pl.when(t < first_up)
        def _():
            to_ring(wo_ref.at[layer, :, cols(t, COLS)])

        u = t - first_up
        is_up = (t >= first_up) & (t < first_down)

        @pl.when(is_up & (lax.rem(u, 2) == 0))
        def _():
            to_ring(wg_ref.at[layer, :, cols(u // 2, COLS)])

        @pl.when(is_up & (lax.rem(u, 2) == 1))
        def _():
            to_ring(wu_ref.at[layer, :, cols(u // 2, COLS)])

        @pl.when((t >= first_down) & (t < first_q))
        def _():
            pltpu.make_async_copy(
                wd_ref.at[layer, :, cols(t - first_down, DOWN_COLS)], ring_down.at[slot], sems.at[slot]
            ).start()

        if has_next:
            @pl.when((t >= first_q) & (t < total))
            def _():
                to_ring(wq_ref.at[layer + 1, :, cols(t - first_q, COLS)])

    def take(t):
        slot = lax.rem(t, LOOKAHEAD)
        pltpu.make_async_copy(wo_ref.at[layer, :, pl.ds(0, COLS)], ring.at[slot], sems.at[slot]).wait()
        return slot

    for t in range(LOOKAHEAD):
        start(jnp.int32(t))
    core = core_ref[0]
    half = oa_ref.shape[1]
    mixed[:, cols(core, half)] = oa_ref[...]
    mixed[:, cols(1 - core, half)] = ob_ref[...]

    def out_body(t, carry):
        slot = take(t)
        attn = jnp.dot(mixed[...], ring[slot], preferred_element_type=F32).astype(BF16)
        out_ref[:, cols(t, COLS)] = (cur_ref[:, cols(t, COLS)].astype(F32) + attn.astype(F32)).astype(BF16)
        start(t + LOOKAHEAD)
        return carry

    lax.fori_loop(0, n_out, out_body, 0)
    norm_into(normed, out_ref, g_mlp_ref)

    def up_body(j, carry):
        t = first_up + 2 * j
        slot = take(t)
        gate = jnp.dot(normed[...], ring[slot], preferred_element_type=F32).astype(BF16)
        inner[:, cols(j, COLS)] = gate
        start(t + LOOKAHEAD)
        slot = take(t + 1)
        up = jnp.dot(normed[...], ring[slot], preferred_element_type=F32).astype(BF16)
        g = inner[:, cols(j, COLS)].astype(F32)
        inner[:, cols(j, COLS)] = (jax.nn.silu(g) * up.astype(F32)).astype(BF16)
        start(t + 1 + LOOKAHEAD)
        return carry

    lax.fori_loop(0, n_up, up_body, 0)

    def down_body(j, carry):
        t = first_down + j
        slot = lax.rem(t, LOOKAHEAD)
        pltpu.make_async_copy(wd_ref.at[layer, :, pl.ds(0, DOWN_COLS)], ring_down.at[slot], sems.at[slot]).wait()
        down = jnp.dot(inner[...], ring_down[slot], preferred_element_type=F32).astype(BF16)
        sl = cols(j, DOWN_COLS)
        out_ref[:, sl] = (out_ref[:, sl].astype(F32) + down.astype(F32)).astype(BF16)
        start(t + LOOKAHEAD)
        return carry

    lax.fori_loop(0, n_down, down_body, 0)
    if has_next:
        norm_into(normed, out_ref, g_next_ref)

        def q_body(j, carry):
            t = first_q + j
            slot = take(t)
            q_ref[:, cols(j, COLS)] = jnp.dot(normed[...], ring[slot], preferred_element_type=F32).astype(BF16)
            start(t + LOOKAHEAD)
            return carry

        lax.fori_loop(0, n_out, q_body, 0)


def layer_dense(core, o_own, o_other, current, g_mlp, g_next, w_o, w_gate, w_up, w_down, w_q, layer, has_next):
    rows, width = current.shape
    hidden = w_gate.shape[2]
    vmem = pl.BlockSpec(memory_space=pltpu.VMEM)
    hbm = pl.BlockSpec(memory_space=pl.ANY)
    row_out = jax.ShapeDtypeStruct((rows, width), BF16)
    n_outs = 2 if has_next else 1
    macs = rows * width * ((2 if has_next else 1) * width + 3 * hidden)
    return pl.pallas_call(
        functools.partial(layer_kernel, layer, has_next),
        in_specs=[pl.BlockSpec(memory_space=pltpu.SMEM)] + [vmem] * 5 + [hbm] * 5,
        out_specs=[vmem] * n_outs,
        out_shape=[row_out] * n_outs,
        scratch_shapes=[
            pltpu.VMEM((rows, width), BF16),
            pltpu.VMEM((rows, width), BF16),
            pltpu.VMEM((rows, hidden), BF16),
            pltpu.VMEM((LOOKAHEAD, width, COLS), BF16),
            pltpu.VMEM((LOOKAHEAD, hidden, DOWN_COLS), BF16),
            pltpu.SemaphoreType.DMA((LOOKAHEAD,)),
        ],
        compiler_params=pltpu.CompilerParams(vmem_limit_bytes=60 * 1024 * 1024),
        cost_estimate=pl.CostEstimate(flops=2 * macs, bytes_accessed=2 * macs // rows, transcendentals=rows * hidden),
        name="layer_dense",
    )(core, o_own, o_other, current, g_mlp, g_next, w_o, w_gate, w_up, w_down, w_q)


def solution(mesh):
    seq_axes = ('sp', 'cp')
    cp_size = mesh.shape['cp']
    devices = mesh.shape['sp'] * cp_size
    row_spec = P(('dp', 'sp', 'cp'), None)
    pairs = [(i, i ^ 1) for i in range(cp_size)]

    def local(hidden, g_kv, w_k, w_v, g_attn, g_mlp, w_q, w_o, w_gate, w_up, w_down):
        rows, width = hidden.shape
        num_layers, n_heads, head_dim = w_o.shape[0], w_o.shape[1], w_o.shape[2]
        half = w_k.shape[1] // 2
        w_o = w_o.reshape(num_layers, n_heads * head_dim, width)
        index = lax.axis_index('sp') * cp_size + lax.axis_index('cp')
        core_id = lax.rem(index, 2).astype(jnp.int32)
        core = core_id.reshape(1)
        info = jnp.stack([core_id, (index // 2).astype(jnp.int32), core_id])

        normed = rms_norm(hidden, g_kv)
        part = rows // KV_CHUNKS
        gathered = [
            lax.all_gather(normed[c * part:(c + 1) * part], seq_axes, axis=0, tiled=True) for c in range(KV_CHUNKS)
        ]
        query = query_project(hidden, g_attn[0:1], w_q, 0)
        kv = None
        for c in range(KV_CHUNKS):
            kv = kv_project(core, gathered[c], w_k, w_v, c, devices, kv)
        keys, values = (a.reshape(devices * rows, half) for a in kv)

        def swap(full_or_half):
            return lax.ppermute(full_or_half, 'cp', pairs)

        current = hidden
        for layer in range(num_layers):
            q_send = lax.dynamic_slice_in_dim(query, (1 - core_id) * half, half, axis=1)
            q_other = swap(q_send)
            o_own, o_send = attention(info, query, q_other, keys, values, head_dim)
            o_other = swap(o_send)
            has_next = layer + 1 < num_layers
            nxt = layer + 1 if has_next else layer
            outs = layer_dense(
                core, o_own, o_other, current, g_mlp[layer:layer + 1], g_attn[nxt:nxt + 1],
                w_o, w_gate, w_up, w_down, w_q, layer, has_next,
            )
            current = outs[0]
            if has_next:
                query = outs[1]
        return current

    return jax.shard_map(local, mesh=mesh, in_specs=(row_spec,) + (P(),) * 10, out_specs=row_spec, check_vma=False)
```

time: 779 us -> 629 us (0.81)
  Pallas kernels: 0 us -> 439 us
  matrix products: 438 us -> 0 us
  waiting for transfers between devices: 245 us -> 162 us
  other arithmetic: 68.3 us -> 5.07 us
    pallas_call x0 -> x9, Pallas kernels: none -> 439 us  [the longest x2 200 us: attention(): pl.pallas_call(functools.partial(attention_kernel, scale), grid_spec=pltp...]
    dot_general x76 -> x0, matrix products: 438 us -> none  [the longest x32 127 us: block_step(): jnp.einsum('trgs,sgd->trgd', probs.astype(jnp.bfloat16), value_block, pre...]
    all_gather x2 -> x4, waiting for transfers between devices: 245 us -> 154 us  [local(): lax.all_gather(normed[c * part:(c + 1) * part], seq_axes, axis=0, tiled=T...]
    reduce_sum x32 -> x0, other arithmetic: 59.7 us -> none  [block_step(): run_sum = run_sum * rescale + jnp.sum(probs, axis=-1)]
  transfers between devices with their start and end apart: 2 -> 8, of which waited for: 2 -> 7; matrix products, arithmetic and copies ran while one was open for 3% -> 0% of each run, Pallas kernels for 0% -> 18%
where the time goes in v1:
time: 629 us
  Pallas kernels  439 us (70%)
  waiting for transfers between devices  162 us (26%)
  between operations  13.2 us (2%)
  local copies, waits for them, and re-layouts  8.36 us (1%)
    pallas_call x2, Pallas kernels, attention(): pl.pallas_call(functools.partial(attention_kernel, scale), grid_spec=pltp...  200 us
    all_gather x4, waiting for transfers between devices, local(): lax.all_gather(normed[c * part:(c + 1) * part], seq_axes, axis=0, tiled=T...  154 us
    pallas_call x2, Pallas kernels, layer_dense(): pl.pallas_call(functools.partial(layer_kernel, layer, has_next), in_specs...  125 us
    pallas_call x4, Pallas kernels, kv_project(): pl.pallas_call(kv_kernel, grid_spec=pltpu.PrefetchScalarGridSpec(num_scal...  104 us
  transfers between devices with their start and end apart: 8, of which 7 were waited for; matrix products, arithmetic and copies ran while one was open for 0% of the time, Pallas kernels for 18%

profile of v1, /device:TPU:29, one launch (start us, length us, event | category | flops | bytes accessed | tf_op | source)
XLA Modules:
  0.0 629.1 jit_solution(7114186761768365949)
XLA Ops:
  6.5 0.0 copy-start.2
  6.5 0.0 all-gather.11.cloned.1.call-start
  6.5 0.7 convert_element_type.10
  7.2 1.8 fusion
  9.1 1.9 fusion.2
  11.0 1.2 fusion.3
  12.2 0.0 all-gather.11.cloned.1.call-update
  12.2 0.0 all-gather.9.cloned.1.call-start
  12.2 0.7 all-gather.9.cloned.1.call-update
  12.9 0.0 all-gather.7.cloned.1.call-start
  13.0 0.7 all-gather.7.cloned.1.call-update
  13.7 0.0 all-gather.5.cloned.1.call-start
  13.7 0.5 all-gather.5.cloned.1.call-update
  14.3 0.0 copy-done.2
  14.3 0.6 fusion.5
  14.9 10.4 %query_project.1.qa_ref = bf16[256,3072]{1,0:T(8,128)(2,1)} custom-call(bf16[256,3072]{1,0:T(8,128)(2,1)} %cur_ref.1, bf16[1,3072]{1,0:T(2,128)(2,1)} %get-tuple-element.40.gain_ref, bf16[2,3072,3072]{2,1,0:T(8,128)(2,1)} %wq_ref.5), custom_call_target="tpu_custom_call" | custom-call | flops 4831838208 | bytes 18874368 | tf_op jit(solution)/shard_map/query_project/pallas_call | solution.py:211
  25.3 1.2 constant_dynamic-slice_fusion.1
  26.5 0.7 collective-permute-start
  27.2 0.7 pad_add_fusion.info_ref
  27.9 45.5 %all-gather.11.cloned.1.call-done.x_ref = bf16[1024,3072]{1,0:T(8,128)(2,1)} async-done(((bf16[64,3072]{1,0:T(8,128)(2,1)}), bf16[1024,3072]{1,0:T(8,128)(2,1)}) %all-gather.11.cloned.1.call-update) | async-done | bytes 6291472 | tf_op jit(solution)/shard_map/all_gather | solution.py:388
  73.4 26.1 %kv_project.4 = (bf16[16,4,64,1536]{3,2,1,0:T(8,128)(2,1)}, bf16[16,4,64,1536]{3,2,1,0:T(8,128)(2,1)}) custom-call(s32[1]{0:T(128)} %bitcast.core_ref, bf16[1024,3072]{1,0:T(8,128)(2,1)} %all-gather.11.cloned.1.call-done.x_ref, bf16[3072,3072]{1,0:T(8,128)(2,1)} %wk_ref.7, bf16[3072,3072]{1,0:T(8,128)(2,1)} %wv_ref.7), custom_call_target="tpu_custom_call" | custom-call | flops 19327352832 | bytes 31457280 | tf_op jit(solution)/shard_map/kv_project/pallas_call | solution.py:51
  99.5 36.3 %all-gather.9.cloned.1.call-done.x_ref = bf16[1024,3072]{1,0:T(8,128)(2,1)} async-done(((bf16[64,3072]{1,0:T(8,128)(2,1)}), bf16[1024,3072]{1,0:T(8,128)(2,1)}) %all-gather.9.cloned.1.call-update) | async-done | bytes 6291472 | tf_op jit(solution)/shard_map/all_gather | solution.py:388
  135.8 26.1 %kv_project.5 = (bf16[16,4,64,1536]{3,2,1,0:T(8,128)(2,1)}, bf16[16,4,64,1536]{3,2,1,0:T(8,128)(2,1)}) custom-call(s32[1]{0:T(128)} %bitcast.core_ref, bf16[1024,3072]{1,0:T(8,128)(2,1)} %all-gather.9.cloned.1.call-done.x_ref, bf16[3072,3072]{1,0:T(8,128)(2,1)} %wk_ref.7, bf16[3072,3072]{1,0:T(8,128)(2,1)} %wv_ref.7, ...), custom_call_target="tpu_custom_call", output_to_operand_aliasing={{0}: (4, {}), {1}: (5, {})} | custom-call | flops 19327352832 | bytes 31457280 | tf_op jit(solution)/shard_map/kv_project/pallas_call | solution.py:51
  161.9 36.3 %all-gather.7.cloned.1.call-done.x_ref = bf16[1024,3072]{1,0:T(8,128)(2,1)} async-done(((bf16[64,3072]{1,0:T(8,128)(2,1)}), bf16[1024,3072]{1,0:T(8,128)(2,1)}) %all-gather.7.cloned.1.call-update) | async-done | bytes 6291472 | tf_op jit(solution)/shard_map/all_gather | solution.py:388
  198.2 26.1 %kv_project.6 = (bf16[16,4,64,1536]{3,2,1,0:T(8,128)(2,1)}, bf16[16,4,64,1536]{3,2,1,0:T(8,128)(2,1)}) custom-call(s32[1]{0:T(128)} %bitcast.core_ref, bf16[1024,3072]{1,0:T(8,128)(2,1)} %all-gather.7.cloned.1.call-done.x_ref, bf16[3072,3072]{1,0:T(8,128)(2,1)} %wk_ref.7, bf16[3072,3072]{1,0:T(8,128)(2,1)} %wv_ref.7, ...), custom_call_target="tpu_custom_call", output_to_operand_aliasing={{0}: (4, {}), {1}: (5, {})} | custom-call | flops 19327352832 | bytes 31457280 | tf_op jit(solution)/shard_map/kv_project/pallas_call | solution.py:51
  224.3 36.2 %all-gather.5.cloned.1.call-done.x_ref = bf16[1024,3072]{1,0:T(8,128)(2,1)} async-done(((bf16[64,3072]{1,0:T(8,128)(2,1)}), bf16[1024,3072]{1,0:T(8,128)(2,1)}) %all-gather.5.cloned.1.call-update) | async-done | bytes 6291472 | tf_op jit(solution)/shard_map/all_gather | solution.py:388
  260.5 26.1 %kv_project.7 = (bf16[16,4,64,1536]{3,2,1,0:T(8,128)(2,1)}, bf16[16,4,64,1536]{3,2,1,0:T(8,128)(2,1)}) custom-call(s32[1]{0:T(128)} %bitcast.core_ref, bf16[1024,3072]{1,0:T(8,128)(2,1)} %all-gather.5.cloned.1.call-done.x_ref, bf16[3072,3072]{1,0:T(8,128)(2,1)} %wk_ref.7, bf16[3072,3072]{1,0:T(8,128)(2,1)} %wv_ref.7, ...), custom_call_target="tpu_custom_call", output_to_operand_aliasing={{0}: (4, {}), {1}: (5, {})} | custom-call | flops 19327352832 | bytes 31457280 | tf_op jit(solution)/shard_map/kv_project/pallas_call | solution.py:51
  286.6 0.0 collective-permute-done.qb_ref
  286.6 0.0 copy-start.4
  286.6 0.9 copy-done.4
  287.5 0.0 copy-start.3
  287.5 99.9 %attention.2 = (bf16[256,1536]{1,0:T(8,128)(2,1)}, bf16[256,1536]{1,0:T(8,128)(2,1)}) custom-call(s32[3]{0:T(128)} %pad_add_fusion.info_ref, bf16[256,3072]{1,0:T(8,128)(2,1)} %query_project.1.qa_ref, bf16[256,1536]{1,0:T(8,128)(2,1)} %copy-done.4, bf16[4096,1536]{1,0:T(8,128)(2,1)} %bitcast.7, bf16[4096,1536]{1,0:T(8,128)(2,1)} %bitcast.9), custom_call_target="tpu_custom_call" | custom-call | flops 12884901888 | bytes 25165824 | tf_op jit(solution)/shard_map/attention/pallas_call | solution.py:145
  387.4 0.3 collective-permute-start.1
  387.7 0.0 copy-done.3
  387.7 0.6 fusion.4
  388.3 1.4 collective-permute-done.1.ob_ref
  389.7 0.0 copy-start
  389.7 0.9 copy-done
  390.5 66.1 %layer_dense.2 = (bf16[256,3072]{1,0:T(8,128)(2,1)}, bf16[256,3072]{1,0:T(8,128)(2,1)}) custom-call(s32[1]{0:T(128)} %bitcast.core_ref, bf16[256,1536]{1,0:T(8,128)(2,1)} %get-tuple-element.27.oa_ref, bf16[256,1536]{1,0:T(8,128)(2,1)} %copy-done, bf16[256,3072]{1,0:T(8,128)(2,1)} %cur_ref.1, bf16[1,3072]{1,0:T(2,128)(2,1)} %get-tuple-element.38.g_mlp_ref, ...), custom_call_target="tpu_custom_call" | custom-call | flops 48318382080 | bytes 188743680 | tf_op jit(solution)/shard_map/layer_dense/pallas_call | solution.py:349
  456.6 1.2 constant_dynamic-slice_fusion
  457.8 0.3 collective-permute-start.2
  458.2 2.0 collective-permute-done.2.qb_ref
  460.2 0.9 copy-done.5
  461.0 99.8 %attention.3 = (bf16[256,1536]{1,0:T(8,128)(2,1)}, bf16[256,1536]{1,0:T(8,128)(2,1)}) custom-call(s32[3]{0:T(128)} %pad_add_fusion.info_ref, bf16[256,3072]{1,0:T(8,128)(2,1)} %get-tuple-element.29.qa_ref, bf16[256,1536]{1,0:T(8,128)(2,1)} %copy-done.5, bf16[4096,1536]{1,0:T(8,128)(2,1)} %bitcast.8, bf16[4096,1536]{1,0:T(8,128)(2,1)} %bitcast.10), custom_call_target="tpu_custom_call" | custom-call | flops 12884901888 | bytes 25165824 | tf_op jit(solution)/shard_map/attention/pallas_call | solution.py:145
  560.8 0.3 collective-permute-start.3
  561.1 2.0 collective-permute-done.3.ob_ref
  563.1 0.9 copy-done.1
  564.0 58.5 %layer_dense.3 = bf16[256,3072]{1,0:T(8,128)(2,1)} custom-call(s32[1]{0:T(128)} %bitcast.core_ref, bf16[256,1536]{1,0:T(8,128)(2,1)} %get-tuple-element.30.oa_ref, bf16[256,1536]{1,0:T(8,128)(2,1)} %copy-done.1, bf16[256,3072]{1,0:T(8,128)(2,1)} %get-tuple-element.32.cur_ref, bf16[1,3072]{1,0:T(2,128)(2,1)} %get-tuple-element.37.g_mlp_ref, ...), custom_call_target="tpu_custom_call" | custom-call | flops 43486543872 | bytes 169869312 | tf_op jit(solution)/shard_map/layer_dense/pallas_call | solution.py:349
  (3 shorter events, 0.0 us)
Async XLA Ops:
  6.5 7.7 %copy-start.2 = (bf16[2,3072]{1,0:T(2,128)(2,1)S(1)}, bf16[2,3072]{1,0:T(2,128)(2,1)}, u32[]{:S(2)}) copy-start(bf16[2,3072]{1,0:T(2,128)(2,1)} %param.15) | copy-start | bytes 36868
  6.5 66.8 %all-gather.11.cloned.1.call-start = ((), (), s32[]{:S(2)}) async-start(), calls=%async_computation.3 | async-start | bytes 6684672 | tf_op jit(solution)/shard_map/all_gather | solution.py:388
  12.2 123.6 %all-gather.9.cloned.1.call-start = ((), (), s32[]{:S(2)}) async-start(), calls=%async_computation.2 | async-start | bytes 6684672 | tf_op jit(solution)/shard_map/all_gather | solution.py:388
  12.9 185.3 %all-gather.7.cloned.1.call-start = ((), (), s32[]{:S(2)}) async-start(), calls=%async_computation.1 | async-start | bytes 6684672 | tf_op jit(solution)/shard_map/all_gather | solution.py:388
  13.7 246.8 %all-gather.5.cloned.1.call-start = ((), (), s32[]{:S(2)}) async-start(), calls=%async_computation | async-start | bytes 6684672 | tf_op jit(solution)/shard_map/all_gather | solution.py:388
  26.5 260.1 %collective-permute-start = (bf16[256,1536]{1,0:T(8,128)(2,1)S(1)}, bf16[256,1536]{1,0:T(8,128)(2,1)S(1)}, u32[]{:S(2)}, u32[]{:S(2)}) collective-permute-start(bf16[256,1536]{1,0:T(8,128)(2,1)S(1)} %constant_dynamic-slice_fusion.1), channel_id=1, source_target_pairs={{0,1},{1,0},{2,3},{3,2},{4,5},{5,4},{6,7},{7,6},{8,9},{9,8},{10,11... | collective-permute-start | bytes 2359304 | tf_op jit(solution)/shard_map/ppermute | solution.py:397
  286.6 0.9 copy-start.4
  287.5 100.2 %copy-start.3 = (bf16[2,3072]{1,0:T(2,128)(2,1)S(1)}, bf16[2,3072]{1,0:T(2,128)(2,1)}, u32[]{:S(2)}) copy-start(bf16[2,3072]{1,0:T(2,128)(2,1)} %param.16) | copy-start | bytes 36868
  387.4 2.3 collective-permute-start.1
  389.7 0.9 copy-start
  457.8 2.4 collective-permute-start.2
  460.2 0.9 copy-start.5
  560.8 2.3 collective-permute-start.3
  563.1 0.9 copy-start.1
Sparse Core Ops, SparseCore 0:
  12.3 61.0 all-gather.10
  75.7 60.0 all-gather.8
  138.1 60.0 all-gather.6
  200.4 60.0 all-gather.4

commit v2 on v0

v2 whole, which is shorter than its diff:
```python
import functools

import jax
import jax.numpy as jnp
from jax import lax
from jax.experimental import pallas as pl
from jax.experimental.pallas import tpu as pltpu
from jax.sharding import PartitionSpec as P

F32 = jnp.float32
BF16 = jnp.bfloat16
MESH = pl.DeviceIdType.MESH
NEG_BIG = -1e30
LOOKAHEAD = 4
WIDE = 768
COLS = 512
DOWN_COLS = 256
LOG2E = 1.4426950408889634
VMEM_LIMIT = 60 * 1024 * 1024


def cols(i, size):
    return pl.ds(pl.multiple_of(i * size, size), size)


def my_index(cp_size):
    return lax.axis_index('sp') * cp_size + lax.axis_index('cp')


def device(i, cp_size):
    return {'sp': i // cp_size, 'cp': lax.rem(i, cp_size)}


def barrier_signal(n, cp_size):
    me = my_index(cp_size)
    barrier = pltpu.get_barrier_semaphore()

    def body(k, carry):
        peer = lax.rem(me + k, n)
        pl.semaphore_signal(barrier, inc=1, device_id=device(peer, cp_size), device_id_type=MESH)
        return carry

    lax.fori_loop(1, n, body, 0)


def barrier_wait(n):
    pl.semaphore_wait(pltpu.get_barrier_semaphore(), n - 1)


def remote(src, dst, send_sem, recv_sem, peer, cp_size):
    return pltpu.make_async_remote_copy(
        src_ref=src, dst_ref=dst, send_sem=send_sem, recv_sem=recv_sem, device_id=device(peer, cp_size), device_id_type=MESH
    )


def send_block(src_of, dst_of, send_sem, recv_sem, local_sem, peer, me, cp_size):
    @pl.when(peer != me)
    def _():
        remote(src_of(peer), dst_of(me), send_sem.at[peer], recv_sem.at[me], peer, cp_size).start()

    @pl.when(peer == me)
    def _():
        pltpu.make_async_copy(src_of(me), dst_of(me), local_sem).start()


def finish_blocks(src_of, dst_of, send_sem, recv_sem, local_sem, me, n, cp_size):
    pltpu.make_async_copy(src_of(me), dst_of(me), local_sem).wait()

    def body(k, carry):
        peer = lax.rem(me + k, n)
        remote(src_of(peer), dst_of(peer), send_sem.at[peer], recv_sem.at[peer], peer, cp_size).wait_send()
        remote(src_of(peer), dst_of(peer), send_sem.at[peer], recv_sem.at[peer], peer, cp_size).wait_recv()
        return carry

    lax.fori_loop(1, n, body, 0)


def norm_into(dst_ref, src_ref, gain_ref):
    rows = src_ref.shape[0]
    gain = gain_ref[...].astype(F32)

    def body(i, carry):
        sl = pl.ds(pl.multiple_of(i * 32, 32), 32)
        wide = src_ref[sl, :].astype(F32)
        inv = lax.rsqrt(jnp.mean(wide * wide, axis=-1, keepdims=True) + 1e-6)
        dst_ref[sl, :] = (wide * inv * gain).astype(BF16)
        return carry

    lax.fori_loop(0, rows // 32, body, 0)


def transposed_tile(normed, weight, buf_of, first):
    out = jnp.dot(normed, weight, preferred_element_type=F32).astype(BF16).T
    size = out.shape[0] // 4
    for j in range(4):
        buf_of(first + j)[...] = out[j * size:(j + 1) * size]


def first_kernel(
    n, cp_size, x_ref, g_kv_ref, g_q_ref, wk_ref, wv_ref, wq_ref, kv_ref, q_ref,
    normed, normed_q, ring, buf, sems, send_sem, recv_sem, local_sem,
):
    me = my_index(cp_size)
    barrier_signal(n, cp_size)
    per = x_ref.shape[1] // WIDE

    def tile_of(t):
        return lax.rem(t + me // cp_size + 1, per)

    def start(t):
        slot = lax.rem(t, LOOKAHEAD)
        for i, w_ref in enumerate((wk_ref, wv_ref)):
            @pl.when(t // per == i)
            def _(w_ref=w_ref):
                pltpu.make_async_copy(w_ref.at[:, cols(tile_of(t), WIDE)], ring.at[slot], sems.at[slot]).start()

        @pl.when(t // per == 2)
        def _():
            pltpu.make_async_copy(wq_ref.at[0, :, cols(tile_of(t), WIDE)], ring.at[slot], sems.at[slot]).start()

    def dst_of(tensor):
        def of(i):
            return q_ref.at[i] if tensor == 2 else kv_ref.at[tensor, i]

        return of

    def send(tensor, t):
        for j in range(4):
            send_block(
                lambda i: buf.at[tensor, i], dst_of(tensor), send_sem.at[tensor], recv_sem.at[tensor],
                local_sem.at[tensor], 4 * tile_of(t) + j, me, cp_size,
            )

    for t in range(LOOKAHEAD):
        start(jnp.int32(t))
    norm_into(normed, x_ref, g_kv_ref)
    norm_into(normed_q, x_ref, g_q_ref)
    barrier_wait(n)
    for tensor in range(3):
        source = normed_q if tensor == 2 else normed

        def body(i, carry, tensor=tensor, source=source):
            t = tensor * per + i
            slot = lax.rem(t, LOOKAHEAD)
            pltpu.make_async_copy(wk_ref.at[:, pl.ds(0, WIDE)], ring.at[slot], sems.at[slot]).wait()
            transposed_tile(source[...], ring[slot], lambda g: buf.at[tensor, g], 4 * tile_of(t))

            @pl.when(i > 0)
            def _():
                send(tensor, t - 1)

            start(t + LOOKAHEAD)
            return carry

        lax.fori_loop(0, per, body, 0)
        if tensor > 0:
            send(tensor - 1, jnp.int32(tensor * per - 1))
    send(2, jnp.int32(3 * per - 1))
    for tensor in range(3):
        finish_blocks(
            lambda i, tensor=tensor: buf.at[tensor, i], dst_of(tensor), send_sem.at[tensor], recv_sem.at[tensor],
            local_sem.at[tensor], me, n, cp_size,
        )


def first_project(n, cp_size, x, g_kv, g_q, w_k, w_v, w_q):
    rows, width = x.shape
    part = width // n
    vmem = pl.BlockSpec(memory_space=pltpu.VMEM)
    hbm = pl.BlockSpec(memory_space=pl.ANY)
    return pl.pallas_call(
        functools.partial(first_kernel, n, cp_size),
        in_specs=[vmem] * 3 + [hbm] * 3,
        out_specs=[hbm] * 2,
        out_shape=[jax.ShapeDtypeStruct((2, n, part, rows), BF16), jax.ShapeDtypeStruct((n, part, rows), BF16)],
        scratch_shapes=[
            pltpu.VMEM((rows, width), BF16),
            pltpu.VMEM((rows, width), BF16),
            pltpu.VMEM((LOOKAHEAD, width, WIDE), BF16),
            pltpu.VMEM((3, n, part, rows), BF16),
            pltpu.SemaphoreType.DMA((LOOKAHEAD,)),
            pltpu.SemaphoreType.DMA((3, n)),
            pltpu.SemaphoreType.DMA((3, n)),
            pltpu.SemaphoreType.DMA((3,)),
        ],
        compiler_params=pltpu.CompilerParams(collective_id=0, has_side_effects=True, vmem_limit_bytes=VMEM_LIMIT),
        cost_estimate=pl.CostEstimate(flops=6 * rows * width * width, bytes_accessed=6 * width * width, transcendentals=0),
        name="first_project",
    )(x, g_kv, g_q, w_k, w_v, w_q)


def attention_kernel(
    n, cp_size, head_dim, q_ref, kv_ref, o_ref, k_nat, m_scr, l_scr, acc_scr, buf, send_sem, recv_sem, local_sem
):
    me = my_index(cp_size)
    barrier_signal(n, cp_size)
    rows = q_ref.shape[2]
    heads = q_ref.shape[1] // head_dim
    span = 2 * rows
    scale = head_dim ** -0.5 * LOG2E

    def flip(u, carry):
        for h in range(heads):
            block = kv_ref[0, u, h * head_dim:(h + 1) * head_dim, :]
            k_nat[h, cols(u, rows), :] = block.T
        return carry

    lax.fori_loop(0, n, flip, 0)
    barrier_wait(n)

    def src_of(i):
        return buf.at[i]

    def dst_of(i):
        return o_ref.at[i]

    def step(t, pair, masked):
        for h in range(heads):
            hs = slice(h * head_dim, (h + 1) * head_dim)
            q_t = q_ref[t, hs, :]
            s = jnp.dot(k_nat[h, cols(pair, span), :], q_t, preferred_element_type=F32) * scale
            if masked:
                key = lax.broadcasted_iota(jnp.int32, s.shape, 0) + pair * span
                query = lax.broadcasted_iota(jnp.int32, s.shape, 1) + t * rows
                s = jnp.where(key <= query, s, NEG_BIG)
            m_old = m_scr[h]
            m_new = jnp.maximum(m_old, jnp.max(s, axis=0, keepdims=True))
            p = jnp.exp2(s - m_new[0:1])
            alpha = jnp.exp2(m_old - m_new)
            m_scr[h] = m_new
            l_scr[h] = l_scr[h] * alpha + jnp.sum(p.reshape(span // 8, 8, rows), axis=0)
            p = p.astype(BF16)
            pv = jnp.dot(kv_ref[1, 2 * pair, hs, :], p[:rows], preferred_element_type=F32)
            pv = pv + jnp.dot(kv_ref[1, 2 * pair + 1, hs, :], p[rows:], preferred_element_type=F32)
            acc_scr[h] = acc_scr[h] * alpha[0:1] + pv

    def block(k, carry):
        t = lax.rem(me + 1 + k, n)
        m_scr[...] = jnp.full(m_scr.shape, NEG_BIG, F32)
        l_scr[...] = jnp.zeros(l_scr.shape, F32)
        acc_scr[...] = jnp.zeros(acc_scr.shape, F32)

        def body(pair, carry):
            step(t, pair, False)
            return carry

        lax.fori_loop(0, t // 2, body, 0)

        @pl.when(k > 0)
        def _():
            send_block(src_of, dst_of, send_sem, recv_sem, local_sem, lax.rem(me + k, n), me, cp_size)

        step(t, t // 2, True)
        for h in range(heads):
            total = jnp.sum(l_scr[h], axis=0, keepdims=True)
            buf[t, h * head_dim:(h + 1) * head_dim, :] = (acc_scr[h] / total).astype(BF16)
        return carry

    lax.fori_loop(0, n, block, 0)
    send_block(src_of, dst_of, send_sem, recv_sem, local_sem, me, me, cp_size)
    finish_blocks(src_of, dst_of, send_sem, recv_sem, local_sem, me, n, cp_size)


def attention(n, cp_size, head_dim, q, kv, collective_id):
    part, rows = q.shape[1], q.shape[2]
    heads = part // head_dim
    vmem = pl.BlockSpec(memory_space=pltpu.VMEM)
    return pl.pallas_call(
        functools.partial(attention_kernel, n, cp_size, head_dim),
        in_specs=[vmem, vmem],
        out_specs=pl.BlockSpec(memory_space=pl.ANY),
        out_shape=jax.ShapeDtypeStruct(q.shape, BF16),
        scratch_shapes=[
            pltpu.VMEM((heads, n * rows, head_dim), BF16),
            pltpu.VMEM((heads, 8, rows), F32),
            pltpu.VMEM((heads, 8, rows), F32),
            pltpu.VMEM((heads, head_dim, rows), F32),
            pltpu.VMEM(q.shape, BF16),
            pltpu.SemaphoreType.DMA((n,)),
            pltpu.SemaphoreType.DMA((n,)),
            pltpu.SemaphoreType.DMA,
        ],
        compiler_params=pltpu.CompilerParams(
            collective_id=collective_id, has_side_effects=True, vmem_limit_bytes=VMEM_LIMIT
        ),
        cost_estimate=pl.CostEstimate(
            flops=2 * n * n * rows * rows * part, bytes_accessed=8 * n * part * rows, transcendentals=n * n * rows * rows
        ),
        name="attention",
    )(q, kv)


def layer_kernel(
    n, cp_size, layer, has_next, ot_ref, cur_ref, g_mlp_ref, g_next_ref, wo_ref, wg_ref, wu_ref, wd_ref, wq_ref, *refs
):
    if has_next:
        out_ref, q_ref, mixed, inner, ring, ring_down, sems, buf, send_sem, recv_sem, local_sem = refs
    else:
        out_ref, mixed, inner, ring, ring_down, sems = refs
    normed = mixed
    rows, width = cur_ref.shape
    hidden = wg_ref.shape[2]
    per = width // WIDE
    n_up = hidden // COLS
    n_down = width // DOWN_COLS
    first_up = per
    first_down = per + 2 * n_up
    first_q = first_down + n_down
    total = first_q + (per if has_next else 0)
    if has_next:
        me = my_index(cp_size)
        barrier_signal(n, cp_size)

    def tile_of(i):
        return lax.rem(i + me // cp_size + 1, per)

    def start(t):
        slot = lax.rem(t, LOOKAHEAD)
        narrow = ring.at[slot, :, pl.ds(0, COLS)]

        @pl.when(t < first_up)
        def _():
            pltpu.make_async_copy(wo_ref.at[layer, :, cols(t, WIDE)], ring.at[slot], sems.at[slot]).start()

        u = t - first_up
        is_up = (t >= first_up) & (t < first_down)

        @pl.when(is_up & (lax.rem(u, 2) == 0))
        def _():
            pltpu.make_async_copy(wg_ref.at[layer, :, cols(u // 2, COLS)], narrow, sems.at[slot]).start()

        @pl.when(is_up & (lax.rem(u, 2) == 1))
        def _():
            pltpu.make_async_copy(wu_ref.at[layer, :, cols(u // 2, COLS)], narrow, sems.at[slot]).start()

        @pl.when((t >= first_down) & (t < first_q))
        def _():
            pltpu.make_async_copy(
                wd_ref.at[layer, :, cols(t - first_down, DOWN_COLS)], ring_down.at[slot], sems.at[slot]
            ).start()

        if has_next:
            @pl.when((t >= first_q) & (t < total))
            def _():
                pltpu.make_async_copy(
                    wq_ref.at[layer + 1, :, cols(tile_of(t - first_q), WIDE)], ring.at[slot], sems.at[slot]
                ).start()

    def take_wide(t):
        slot = lax.rem(t, LOOKAHEAD)
        pltpu.make_async_copy(wo_ref.at[layer, :, pl.ds(0, WIDE)], ring.at[slot], sems.at[slot]).wait()
        return ring[slot]

    def take(t):
        slot = lax.rem(t, LOOKAHEAD)
        narrow = ring.at[slot, :, pl.ds(0, COLS)]
        pltpu.make_async_copy(wg_ref.at[layer, :, pl.ds(0, COLS)], narrow, sems.at[slot]).wait()
        return narrow[...]

    for t in range(LOOKAHEAD):
        start(jnp.int32(t))

    def flip(i, carry):
        mixed[:, cols(i, 256)] = ot_ref[cols(i, 256), :].T
        return carry

    lax.fori_loop(0, width // 256, flip, 0)

    def out_body(t, carry):
        attn = jnp.dot(mixed[...], take_wide(t), preferred_element_type=F32).astype(BF16)
        out_ref[:, cols(t, WIDE)] = (cur_ref[:, cols(t, WIDE)].astype(F32) + attn.astype(F32)).astype(BF16)
        start(t + LOOKAHEAD)
        return carry

    lax.fori_loop(0, per, out_body, 0)
    norm_into(normed, out_ref, g_mlp_ref)

    def up_body(j, carry):
        t = first_up + 2 * j
        inner[:, cols(j, COLS)] = jnp.dot(normed[...], take(t), preferred_element_type=F32).astype(BF16)
        start(t + LOOKAHEAD)
        up = jnp.dot(normed[...], take(t + 1), preferred_element_type=F32).astype(BF16)
        g = inner[:, cols(j, COLS)].astype(F32)
        inner[:, cols(j, COLS)] = (jax.nn.silu(g) * up.astype(F32)).astype(BF16)
        start(t + 1 + LOOKAHEAD)
        return carry

    lax.fori_loop(0, n_up, up_body, 0)

    def down_body(j, carry):
        t = first_down + j
        slot = lax.rem(t, LOOKAHEAD)
        pltpu.make_async_copy(wd_ref.at[layer, :, pl.ds(0, DOWN_COLS)], ring_down.at[slot], sems.at[slot]).wait()
        down = jnp.dot(inner[...], ring_down[slot], preferred_element_type=F32).astype(BF16)
        sl = cols(j, DOWN_COLS)
        out_ref[:, sl] = (out_ref[:, sl].astype(F32) + down.astype(F32)).astype(BF16)
        start(t + LOOKAHEAD)
        return carry

    lax.fori_loop(0, n_down, down_body, 0)
    if has_next:
        norm_into(normed, out_ref, g_next_ref)
        barrier_wait(n)

        def src_of(i):
            return buf.at[i]

        def dst_of(i):
            return q_ref.at[i]

        def send(i):
            for j in range(4):
                send_block(src_of, dst_of, send_sem, recv_sem, local_sem, 4 * tile_of(i) + j, me, cp_size)

        def q_body(i, carry):
            transposed_tile(normed[...], take_wide(first_q + i), src_of, 4 * tile_of(i))

            @pl.when(i > 0)
            def _():
                send(i - 1)

            return carry

        lax.fori_loop(0, per, q_body, 0)
        send(jnp.int32(per - 1))
        finish_blocks(src_of, dst_of, send_sem, recv_sem, local_sem, me, n, cp_size)


def layer_dense(n, cp_size, o_t, current, g_mlp, g_next, w_o, w_gate, w_up, w_down, w_q, layer, has_next, collective_id):
    rows, width = current.shape
    hidden = w_gate.shape[2]
    part = width // n
    vmem = pl.BlockSpec(memory_space=pltpu.VMEM)
    hbm = pl.BlockSpec(memory_space=pl.ANY)
    out_shape = [jax.ShapeDtypeStruct((rows, width), BF16)]
    out_specs = [vmem]
    scratch = [
        pltpu.VMEM((rows, width), BF16),
        pltpu.VMEM((rows, hidden), BF16),
        pltpu.VMEM((LOOKAHEAD, width, WIDE), BF16),
        pltpu.VMEM((LOOKAHEAD, hidden, DOWN_COLS), BF16),
        pltpu.SemaphoreType.DMA((LOOKAHEAD,)),
    ]
    params = dict(vmem_limit_bytes=VMEM_LIMIT)
    if has_next:
        out_shape.append(jax.ShapeDtypeStruct((n, part, rows), BF16))
        out_specs.append(hbm)
        scratch += [
            pltpu.VMEM((n, part, rows), BF16),
            pltpu.SemaphoreType.DMA((n,)),
            pltpu.SemaphoreType.DMA((n,)),
            pltpu.SemaphoreType.DMA,
        ]
        params.update(collective_id=collective_id, has_side_effects=True)
    macs = rows * width * ((2 if has_next else 1) * width + 3 * hidden)
    return pl.pallas_call(
        functools.partial(layer_kernel, n, cp_size, layer, has_next),
        in_specs=[vmem] * 4 + [hbm] * 5,
        out_specs=out_specs,
        out_shape=out_shape,
        scratch_shapes=scratch,
        compiler_params=pltpu.CompilerParams(**params),
        cost_estimate=pl.CostEstimate(flops=2 * macs, bytes_accessed=2 * macs // rows, transcendentals=rows * hidden),
        name="layer_dense",
    )(o_t, current, g_mlp, g_next, w_o, w_gate, w_up, w_down, w_q)


def solution(mesh):
    cp_size = mesh.shape['cp']
    n = mesh.shape['sp'] * cp_size
    row_spec = P(('dp', 'sp', 'cp'), None)

    def local(hidden, g_kv, w_k, w_v, g_attn, g_mlp, w_q, w_o, w_gate, w_up, w_down):
        rows, width = hidden.shape
        num_layers, n_heads, head_dim = w_o.shape[0], w_o.shape[1], w_o.shape[2]
        w_o = w_o.reshape(num_layers, n_heads * head_dim, width)
        kv, query = first_project(n, cp_size, hidden, g_kv.reshape(1, width), g_attn[0:1], w_k, w_v, w_q)
        current = hidden
        for layer in range(num_layers):
            o_t = attention(n, cp_size, head_dim, query, kv, 2 * layer + 1).reshape(width, rows)
            has_next = layer + 1 < num_layers
            nxt = layer + 1 if has_next else layer
            outs = layer_dense(
                n, cp_size, o_t, current, g_mlp[layer:layer + 1], g_attn[nxt:nxt + 1],
                w_o, w_gate, w_up, w_down, w_q, layer, has_next, 2 * layer + 2,
            )
            current = outs[0]
            if has_next:
                query = outs[1]
        return current

    return jax.shard_map(local, mesh=mesh, in_specs=(row_spec,) + (P(),) * 10, out_specs=row_spec, check_vma=False)
```

time: 779 us -> 439 us (0.56)
  matrix products: 438 us -> 0 us
  Pallas kernels: 0 us -> 435 us
  waiting for transfers between devices: 245 us -> 0 us
  other arithmetic: 68.3 us -> 0 us
  between operations: 13.9 us -> 0.19 us
    dot_general x76 -> x0, matrix products: 438 us -> none  [the longest x32 127 us: block_step(): jnp.einsum('trgs,sgd->trgd', probs.astype(jnp.bfloat16), value_block, pre...]
    pallas_call x0 -> x5, Pallas kernels: none -> 435 us  [the longest x2 162 us: layer_dense(): pl.pallas_call(functools.partial(layer_kernel, n, cp_size, layer, has_nex...]
    all_gather x2 -> x0, waiting for transfers between devices: 245 us -> none  [the longest x1 135 us: local(): values_all = lax.all_gather(values_local, seq_axes, axis=0, tiled=True)]
    reduce_sum x33 -> x0, other arithmetic: 61.5 us -> none  [the longest x32 59.7 us: block_step(): run_sum = run_sum * rescale + jnp.sum(probs, axis=-1)]
  transfers between devices with their start and end apart: 2 -> 0, of which waited for: 2 -> 0; matrix products, arithmetic and copies ran while one was open for 3% -> 0% of each run, Pallas kernels for 0% -> 0%
where the time goes in v2:
time: 439 us; the launch traced here: 437 us
  Pallas kernels  435 us (99%)
    pallas_call x2, Pallas kernels, layer_dense(): pl.pallas_call(functools.partial(layer_kernel, n, cp_size, layer, has_nex...  162 us
    pallas_call x2, Pallas kernels, attention(): pl.pallas_call(functools.partial(attention_kernel, n, cp_size, head_dim),...  160 us
    pallas_call x1, Pallas kernels, first_project(): pl.pallas_call(functools.partial(first_kernel, n, cp_size), in_specs=[vme...  113 us

profile of v2, /device:TPU:29, one launch (start us, length us, event | category | flops | bytes accessed | tf_op | source)
XLA Modules:
  0.0 437.5 jit_solution(2831984528064538959)
XLA Ops:
  0.0 1.3 reshape.12.g_kv_ref
  1.3 1.4 fusion
  2.7 112.5 %first_project.1 = (bf16[2,16,192,256]{3,2,1,0:T(8,128)(2,1)}, bf16[16,192,256]{2,1,0:T(8,128)(2,1)}) custom-call(bf16[256,3072]{1,0:T(8,128)(2,1)} %cur_ref.1, bf16[1,3072]{1,0:T(2,128)(2,1)} %reshape.12.g_kv_ref, bf16[1,3072]{1,0:T(2,128)(2,1)} %get-tuple-element.17.g_q_ref, bf16[3072,3072]{1,0:T(8,128)(2,1)} %wk_ref.1, bf16[3072,3072]{1,0:T(8,128)(2,1)} %wv_ref.1, ...), custom_call_target="tpu_custom_call" | custom-call | flops 14495514624 | bytes 56623104 | tf_op jit(solution)/shard_map/first_project/pallas_call | solution.py:171
  115.3 80.0 %attention.2 = bf16[16,192,256]{2,1,0:T(8,128)(2,1)} custom-call(bf16[16,192,256]{2,1,0:T(8,128)(2,1)} %get-tuple-element.9.q_ref, bf16[2,16,192,256]{3,2,1,0:T(8,128)(2,1)} %get-tuple-element.10.kv_ref), custom_call_target="tpu_custom_call" | custom-call | flops 6442450944 | bytes 6291456 | tf_op jit(solution)/shard_map/attention/pallas_call | solution.py:268
  195.4 99.9 %layer_dense.2 = (bf16[256,3072]{1,0:T(8,128)(2,1)}, bf16[16,192,256]{2,1,0:T(8,128)(2,1)}) custom-call(bf16[3072,256]{1,0:T(8,128)(2,1)} %bitcast.6, bf16[256,3072]{1,0:T(8,128)(2,1)} %cur_ref.1, bf16[1,3072]{1,0:T(2,128)(2,1)} %get-tuple-element.14.g_mlp_ref, bf16[1,3072]{1,0:T(2,128)(2,1)} %get-tuple-element.18.g_next_ref, ...), custom_call_target="tpu_custom_call" | custom-call | flops 48318382080 | bytes 188743680 | tf_op jit(solution)/shard_map/layer_dense/pallas_call | solution.py:456
  295.2 80.1 %attention.3 = bf16[16,192,256]{2,1,0:T(8,128)(2,1)} custom-call(bf16[16,192,256]{2,1,0:T(8,128)(2,1)} %get-tuple-element.11.q_ref, bf16[2,16,192,256]{3,2,1,0:T(8,128)(2,1)} %get-tuple-element.10.kv_ref), custom_call_target="tpu_custom_call" | custom-call | flops 6442450944 | bytes 6291456 | tf_op jit(solution)/shard_map/attention/pallas_call | solution.py:268
  375.3 62.0 %layer_dense.3 = bf16[256,3072]{1,0:T(8,128)(2,1)} custom-call(bf16[3072,256]{1,0:T(8,128)(2,1)} %bitcast.5, bf16[256,3072]{1,0:T(8,128)(2,1)} %get-tuple-element.12.cur_ref, bf16[1,3072]{1,0:T(2,128)(2,1)} %get-tuple-element.13.g_mlp_ref, bf16[1,3072]{1,0:T(2,128)(2,1)} %get-tuple-element.18.g_next_ref, bf16[2,3072,3072]{2,1,0:T(8,128)(2,1)} %bitcast.4, ...), custom_call_target="tpu_custom_call" | custom-call | flops 43486543872 | bytes 169869312 | tf_op jit(solution)/shard_map/layer_dense/pallas_call | solution.py:456

commit v3 on v2

--- a/solution.py
+++ b/solution.py
@@ -190,7 +190,8 @@
 
 
 def attention_kernel(
-    n, cp_size, head_dim, q_ref, kv_ref, o_ref, k_nat, m_scr, l_scr, acc_scr, buf, send_sem, recv_sem, local_sem
+    n, cp_size, head_dim, q_ref, kv_ref, o_ref, k_nat, v_all, s_scr, top_scr, max_scr, sum_scr, acc_scr, buf,
+    send_sem, recv_sem, local_sem,
 ):
     me = my_index(cp_size)
     barrier_signal(n, cp_size)
@@ -201,12 +202,12 @@
 
     def flip(u, carry):
         for h in range(heads):
-            block = kv_ref[0, u, h * head_dim:(h + 1) * head_dim, :]
-            k_nat[h, cols(u, rows), :] = block.T
+            hs = slice(h * head_dim, (h + 1) * head_dim)
+            k_nat[h, cols(u, rows), :] = kv_ref[0, u, hs, :].T
+            v_all[h, :, cols(u, rows)] = kv_ref[1, u, hs, :]
         return carry
 
     lax.fori_loop(0, n, flip, 0)
-    barrier_wait(n)
 
     def src_of(i):
         return buf.at[i]
@@ -214,50 +215,92 @@
     def dst_of(i):
         return o_ref.at[i]
 
-    def step(t, pair, masked):
+    def block_of(k):
+        return lax.rem(me + 1 + k, n)
+
+    def scores(k, pair, masked):
+        t = block_of(k)
+        slot = lax.rem(k, 2)
         for h in range(heads):
-            hs = slice(h * head_dim, (h + 1) * head_dim)
-            q_t = q_ref[t, hs, :]
-            s = jnp.dot(k_nat[h, cols(pair, span), :], q_t, preferred_element_type=F32) * scale
+            q_t = q_ref[t, h * head_dim:(h + 1) * head_dim, :]
+            s = jnp.dot(k_nat[h, cols(pair, span), :], q_t, preferred_element_type=F32)
             if masked:
                 key = lax.broadcasted_iota(jnp.int32, s.shape, 0) + pair * span
                 query = lax.broadcasted_iota(jnp.int32, s.shape, 1) + t * rows
                 s = jnp.where(key <= query, s, NEG_BIG)
-            m_old = m_scr[h]
-            m_new = jnp.maximum(m_old, jnp.max(s, axis=0, keepdims=True))
-            p = jnp.exp2(s - m_new[0:1])
-            alpha = jnp.exp2(m_old - m_new)
-            m_scr[h] = m_new
-            l_scr[h] = l_scr[h] * alpha + jnp.sum(p.reshape(span // 8, 8, rows), axis=0)
-            p = p.astype(BF16)
-            pv = jnp.dot(kv_ref[1, 2 * pair, hs, :], p[:rows], preferred_element_type=F32)
-            pv = pv + jnp.dot(kv_ref[1, 2 * pair + 1, hs, :], p[rows:], preferred_element_type=F32)
-            acc_scr[h] = acc_scr[h] * alpha[0:1] + pv
+            s_scr[slot, h, cols(pair, span), :] = s
+            top = jnp.max(s.reshape(span // 8, 8, rows), axis=0)
+            top_scr[slot, h] = jnp.maximum(top_scr[slot, h], top)
+
+    def values(k, pair):
+        slot = lax.rem(k, 2)
+        for h in range(heads):
+            s = s_scr[slot, h, cols(pair, span), :].reshape(span // 8, 8, rows)
+            p = jnp.exp2(s * scale - max_scr[h][None])
+            sum_scr[h] = sum_scr[h] + jnp.sum(p, axis=0)
+            p = p.reshape(span, rows).astype(BF16)
+            acc_scr[h] = acc_scr[h] + jnp.dot(v_all[h, :, cols(pair, span)], p, preferred_element_type=F32)
+
+    def loop(lo, hi, fn):
+        def body(pair, carry):
+            fn(pair)
+            return carry
+
+        lax.fori_loop(lo, hi, body, 0)
+
+    def clear_top(k):
+        top_scr[lax.rem(k, 2)] = jnp.full(top_scr.shape[1:], NEG_BIG, F32)
+
+    clear_top(jnp.int32(0))
+    loop(0, block_of(0) // 2, lambda pair: scores(0, pair, False))
+    scores(0, block_of(0) // 2, True)
+    barrier_wait(n)
+
+    def begin_values(k):
+        for h in range(heads):
+            top = jnp.max(top_scr[lax.rem(k, 2), h], axis=0, keepdims=True) * scale
+            max_scr[h] = jnp.broadcast_to(top, max_scr.shape[1:])
+        sum_scr[...] = jnp.zeros(sum_scr.shape, F32)
+        acc_scr[...] = jnp.zeros(acc_scr.shape, F32)
+
+    def end_values(k):
+        for h in range(heads):
+            total = jnp.sum(sum_scr[h], axis=0, keepdims=True)
+            buf[block_of(k), h * head_dim:(h + 1) * head_dim, :] = (acc_scr[h] / total).astype(BF16)
+
+    def send(k):
+        send_block(src_of, dst_of, send_sem, recv_sem, local_sem, block_of(k), me, cp_size)
 
     def block(k, carry):
-        t = lax.rem(me + 1 + k, n)
-        m_scr[...] = jnp.full(m_scr.shape, NEG_BIG, F32)
-        l_scr[...] = jnp.zeros(l_scr.shape, F32)
-        acc_scr[...] = jnp.zeros(acc_scr.shape, F32)
-
-        def body(pair, carry):
-            step(t, pair, False)
-            return carry
-
-        lax.fori_loop(0, t // 2, body, 0)
+        last = block_of(k) // 2
+        last_next = block_of(k + 1) // 2
+        begin_values(k)
+        clear_top(k + 1)
+        both = jnp.minimum(last, last_next)
+
+        def fused(pair):
+            scores(k + 1, pair, False)
+            values(k, pair)
+
+        loop(0, both, fused)
 
         @pl.when(k > 0)
         def _():
-            send_block(src_of, dst_of, send_sem, recv_sem, local_sem, lax.rem(me + k, n), me, cp_size)
-
-        step(t, t // 2, True)
-        for h in range(heads):
-            total = jnp.sum(l_scr[h], axis=0, keepdims=True)
-            buf[t, h * head_dim:(h + 1) * head_dim, :] = (acc_scr[h] / total).astype(BF16)
-        return carry
-
-    lax.fori_loop(0, n, block, 0)
-    send_block(src_of, dst_of, send_sem, recv_sem, local_sem, me, me, cp_size)
+            send(k - 1)
+
+        loop(both, last, lambda pair: values(k, pair))
+        loop(both, last_next, lambda pair: scores(k + 1, pair, False))
+        scores(k + 1, last_next, True)
+        values(k, last)
+        end_values(k)
+        return carry
+
+    lax.fori_loop(0, n - 1, block, 0)
+    begin_values(n - 1)
+    send(n - 2)
+    loop(0, me // 2 + 1, lambda pair: values(n - 1, pair))
+    end_values(n - 1)
+    send(n - 1)
     finish_blocks(src_of, dst_of, send_sem, recv_sem, local_sem, me, n, cp_size)
 
 
@@ -272,6 +315,9 @@
         out_shape=jax.ShapeDtypeStruct(q.shape, BF16),
         scratch_shapes=[
             pltpu.VMEM((heads, n * rows, head_dim), BF16),
+            pltpu.VMEM((heads, head_dim, n * rows), BF16),
+            pltpu.VMEM((2, heads, n * rows, rows), F32),
+            pltpu.VMEM((2, heads, 8, rows), F32),
             pltpu.VMEM((heads, 8, rows), F32),
             pltpu.VMEM((heads, 8, rows), F32),
             pltpu.VMEM((heads, head_dim, rows), F32),

time: 439 us -> 393 us (0.90)
  Pallas kernels: 435 us -> 390 us
    pallas_call x2, Pallas kernels: 160 us -> 116 us  [attention(): pl.pallas_call(functools.partial(attention_kernel, n, cp_size, head_dim),...]
where the time goes in v3:
time: 393 us
  Pallas kernels  390 us (99%)
    pallas_call x2, Pallas kernels, layer_dense(): pl.pallas_call(functools.partial(layer_kernel, n, cp_size, layer, has_nex...  161 us
    pallas_call x2, Pallas kernels, attention(): pl.pallas_call(functools.partial(attention_kernel, n, cp_size, head_dim),...  116 us
    pallas_call x1, Pallas kernels, first_project(): pl.pallas_call(functools.partial(first_kernel, n, cp_size), in_specs=[vme...  113 us

profile of v3, /device:TPU:29, one launch (start us, length us, event | category | flops | bytes accessed | tf_op | source)
XLA Modules:
  0.0 393.2 jit_solution(16567713162940298500)
XLA Ops:
  0.0 1.3 reshape.12.g_kv_ref
  1.3 1.4 fusion
  2.7 112.5 %first_project.1 = (bf16[2,16,192,256]{3,2,1,0:T(8,128)(2,1)}, bf16[16,192,256]{2,1,0:T(8,128)(2,1)}) custom-call(bf16[256,3072]{1,0:T(8,128)(2,1)} %cur_ref.1, bf16[1,3072]{1,0:T(2,128)(2,1)} %reshape.12.g_kv_ref, bf16[1,3072]{1,0:T(2,128)(2,1)} %get-tuple-element.17.g_q_ref, bf16[3072,3072]{1,0:T(8,128)(2,1)} %wk_ref.1, bf16[3072,3072]{1,0:T(8,128)(2,1)} %wv_ref.1, ...), custom_call_target="tpu_custom_call" | custom-call | flops 14495514624 | bytes 56623104 | tf_op jit(solution)/shard_map/first_project/pallas_call | solution.py:171
  115.3 58.2 %attention.2 = bf16[16,192,256]{2,1,0:T(8,128)(2,1)} custom-call(bf16[16,192,256]{2,1,0:T(8,128)(2,1)} %get-tuple-element.9.q_ref, bf16[2,16,192,256]{3,2,1,0:T(8,128)(2,1)} %get-tuple-element.10.kv_ref), custom_call_target="tpu_custom_call" | custom-call | flops 6442450944 | bytes 6291456 | tf_op jit(solution)/shard_map/attention/pallas_call | solution.py:311
  173.5 99.2 %layer_dense.2 = (bf16[256,3072]{1,0:T(8,128)(2,1)}, bf16[16,192,256]{2,1,0:T(8,128)(2,1)}) custom-call(bf16[3072,256]{1,0:T(8,128)(2,1)} %bitcast.6, bf16[256,3072]{1,0:T(8,128)(2,1)} %cur_ref.1, bf16[1,3072]{1,0:T(2,128)(2,1)} %get-tuple-element.14.g_mlp_ref, bf16[1,3072]{1,0:T(2,128)(2,1)} %get-tuple-element.18.g_next_ref, ...), custom_call_target="tpu_custom_call" | custom-call | flops 48318382080 | bytes 188743680 | tf_op jit(solution)/shard_map/layer_dense/pallas_call | solution.py:502
  272.8 58.2 %attention.3 = bf16[16,192,256]{2,1,0:T(8,128)(2,1)} custom-call(bf16[16,192,256]{2,1,0:T(8,128)(2,1)} %get-tuple-element.11.q_ref, bf16[2,16,192,256]{3,2,1,0:T(8,128)(2,1)} %get-tuple-element.10.kv_ref), custom_call_target="tpu_custom_call" | custom-call | flops 6442450944 | bytes 6291456 | tf_op jit(solution)/shard_map/attention/pallas_call | solution.py:311
  331.0 62.0 %layer_dense.3 = bf16[256,3072]{1,0:T(8,128)(2,1)} custom-call(bf16[3072,256]{1,0:T(8,128)(2,1)} %bitcast.5, bf16[256,3072]{1,0:T(8,128)(2,1)} %get-tuple-element.12.cur_ref, bf16[1,3072]{1,0:T(2,128)(2,1)} %get-tuple-element.13.g_mlp_ref, bf16[1,3072]{1,0:T(2,128)(2,1)} %get-tuple-element.18.g_next_ref, bf16[2,3072,3072]{2,1,0:T(8,128)(2,1)} %bitcast.4, ...), custom_call_target="tpu_custom_call" | custom-call | flops 43486543872 | bytes 169869312 | tf_op jit(solution)/shard_map/layer_dense/pallas_call | solution.py:502

commit v4 on v3

--- a/solution.py
+++ b/solution.py
@@ -75,9 +75,9 @@
     lax.fori_loop(1, n, body, 0)
 
 
-def norm_into(dst_ref, src_ref, gain_ref):
+def norm_into(dst_ref, src_ref, gain):
     rows = src_ref.shape[0]
-    gain = gain_ref[...].astype(F32)
+    gain = gain.astype(F32)
 
     def body(i, carry):
         sl = pl.ds(pl.multiple_of(i * 32, 32), 32)
@@ -128,13 +128,13 @@
         for j in range(4):
             send_block(
                 lambda i: buf.at[tensor, i], dst_of(tensor), send_sem.at[tensor], recv_sem.at[tensor],
-                local_sem.at[tensor], 4 * tile_of(t) + j, me, cp_size,
+                local_sem.at[tensor], 4 * tile_of(t) + lax.rem(me + j, 4), me, cp_size,
             )
 
     for t in range(LOOKAHEAD):
         start(jnp.int32(t))
-    norm_into(normed, x_ref, g_kv_ref)
-    norm_into(normed_q, x_ref, g_q_ref)
+    norm_into(normed, x_ref, g_kv_ref[...].reshape(1, x_ref.shape[1]))
+    norm_into(normed_q, x_ref, g_q_ref[0:1, :])
     barrier_wait(n)
     for tensor in range(3):
         source = normed_q if tensor == 2 else normed
@@ -215,8 +215,12 @@
     def dst_of(i):
         return o_ref.at[i]
 
+    side = n // 2
+    mine = me // side
+
     def block_of(k):
-        return lax.rem(me + 1 + k, n)
+        near = k // side
+        return ((1 - mine) * (1 - near) + mine * near) * side + lax.rem(me + k + near, side)
 
     def scores(k, pair, masked):
         t = block_of(k)
@@ -340,9 +344,9 @@
     n, cp_size, layer, has_next, ot_ref, cur_ref, g_mlp_ref, g_next_ref, wo_ref, wg_ref, wu_ref, wd_ref, wq_ref, *refs
 ):
     if has_next:
-        out_ref, q_ref, mixed, inner, ring, ring_down, sems, buf, send_sem, recv_sem, local_sem = refs
+        out_ref, q_ref, mixed, ot_scr, inner, ring, ring_down, sems, in_sems, buf, send_sem, recv_sem, local_sem = refs
     else:
-        out_ref, mixed, inner, ring, ring_down, sems = refs
+        out_ref, mixed, ot_scr, inner, ring, ring_down, sems, in_sems = refs
     normed = mixed
     rows, width = cur_ref.shape
     hidden = wg_ref.shape[2]
@@ -403,23 +407,30 @@
         pltpu.make_async_copy(wg_ref.at[layer, :, pl.ds(0, COLS)], narrow, sems.at[slot]).wait()
         return narrow[...]
 
-    for t in range(LOOKAHEAD):
+    ot_copy = pltpu.make_async_copy(ot_ref, ot_scr, in_sems.at[0])
+    cur_copy = pltpu.make_async_copy(cur_ref, out_ref, in_sems.at[1])
+    ot_copy.start()
+    start(jnp.int32(0))
+    cur_copy.start()
+    for t in range(1, LOOKAHEAD):
         start(jnp.int32(t))
+    ot_copy.wait()
 
     def flip(i, carry):
-        mixed[:, cols(i, 256)] = ot_ref[cols(i, 256), :].T
+        mixed[:, cols(i, 256)] = ot_scr[cols(i, 256), :].T
         return carry
 
     lax.fori_loop(0, width // 256, flip, 0)
+    cur_copy.wait()
 
     def out_body(t, carry):
         attn = jnp.dot(mixed[...], take_wide(t), preferred_element_type=F32).astype(BF16)
-        out_ref[:, cols(t, WIDE)] = (cur_ref[:, cols(t, WIDE)].astype(F32) + attn.astype(F32)).astype(BF16)
+        out_ref[:, cols(t, WIDE)] = (out_ref[:, cols(t, WIDE)].astype(F32) + attn.astype(F32)).astype(BF16)
         start(t + LOOKAHEAD)
         return carry
 
     lax.fori_loop(0, per, out_body, 0)
-    norm_into(normed, out_ref, g_mlp_ref)
+    norm_into(normed, out_ref, g_mlp_ref[layer:layer + 1, :])
 
     def up_body(j, carry):
         t = first_up + 2 * j
@@ -445,7 +456,7 @@
 
     lax.fori_loop(0, n_down, down_body, 0)
     if has_next:
-        norm_into(normed, out_ref, g_next_ref)
+        norm_into(normed, out_ref, g_next_ref[layer + 1:layer + 2, :])
         barrier_wait(n)
 
         def src_of(i):
@@ -456,7 +467,8 @@
 
         def send(i):
             for j in range(4):
-                send_block(src_of, dst_of, send_sem, recv_sem, local_sem, 4 * tile_of(i) + j, me, cp_size)
+                peer = 4 * tile_of(i) + lax.rem(me + j, 4)
+                send_block(src_of, dst_of, send_sem, recv_sem, local_sem, peer, me, cp_size)
 
         def q_body(i, carry):
             transposed_tile(normed[...], take_wide(first_q + i), src_of, 4 * tile_of(i))
@@ -482,10 +494,12 @@
     out_specs = [vmem]
     scratch = [
         pltpu.VMEM((rows, width), BF16),
+        pltpu.VMEM((width, rows), BF16),
         pltpu.VMEM((rows, hidden), BF16),
         pltpu.VMEM((LOOKAHEAD, width, WIDE), BF16),
         pltpu.VMEM((LOOKAHEAD, hidden, DOWN_COLS), BF16),
         pltpu.SemaphoreType.DMA((LOOKAHEAD,)),
+        pltpu.SemaphoreType.DMA((2,)),
     ]
     params = dict(vmem_limit_bytes=VMEM_LIMIT)
     if has_next:
@@ -501,7 +515,7 @@
     macs = rows * width * ((2 if has_next else 1) * width + 3 * hidden)
     return pl.pallas_call(
         functools.partial(layer_kernel, n, cp_size, layer, has_next),
-        in_specs=[vmem] * 4 + [hbm] * 5,
+        in_specs=[hbm] * 2 + [vmem] * 2 + [hbm] * 5,
         out_specs=out_specs,
         out_shape=out_shape,
         scratch_shapes=scratch,
@@ -520,14 +534,13 @@
         rows, width = hidden.shape
         num_layers, n_heads, head_dim = w_o.shape[0], w_o.shape[1], w_o.shape[2]
         w_o = w_o.reshape(num_layers, n_heads * head_dim, width)
-        kv, query = first_project(n, cp_size, hidden, g_kv.reshape(1, width), g_attn[0:1], w_k, w_v, w_q)
+        kv, query = first_project(n, cp_size, hidden, g_kv, g_attn, w_k, w_v, w_q)
         current = hidden
         for layer in range(num_layers):
             o_t = attention(n, cp_size, head_dim, query, kv, 2 * layer + 1).reshape(width, rows)
             has_next = layer + 1 < num_layers
-            nxt = layer + 1 if has_next else layer
             outs = layer_dense(
-                n, cp_size, o_t, current, g_mlp[layer:layer + 1], g_attn[nxt:nxt + 1],
+                n, cp_size, o_t, current, g_mlp, g_attn,
                 w_o, w_gate, w_up, w_down, w_q, layer, has_next, 2 * layer + 2,
             )
             current = outs[0]

time: 393 us -> 391 us (level); the launches traced: 393 us -> 387 us
    pallas_call x2, Pallas kernels: 116 us -> 103 us  [attention(): pl.pallas_call(functools.partial(attention_kernel, n, cp_size, head_dim),...]
    pallas_call x2, Pallas kernels: 161 us -> 171 us  [layer_dense(): pl.pallas_call(functools.partial(layer_kernel, n, cp_size, layer, has_nex...]
where the time goes in v4:
time: 391 us; the launch traced here: 387 us
  Pallas kernels  387 us (99%)
    pallas_call x2, Pallas kernels, layer_dense(): pl.pallas_call(functools.partial(layer_kernel, n, cp_size, layer, has_nex...  171 us
    pallas_call x1, Pallas kernels, first_project(): pl.pallas_call(functools.partial(first_kernel, n, cp_size), in_specs=[vme...  112 us
    pallas_call x2, Pallas kernels, attention(): pl.pallas_call(functools.partial(attention_kernel, n, cp_size, head_dim),...  103 us

profile of v4, /device:TPU:29, one launch (start us, length us, event | category | flops | bytes accessed | tf_op | source)
XLA Modules:
  0.0 386.7 jit_solution(5611961350721381645)
XLA Ops:
  0.0 112.4 %first_project.1 = (bf16[2,16,192,256]{3,2,1,0:T(8,128)(2,1)}, bf16[16,192,256]{2,1,0:T(8,128)(2,1)}) custom-call(bf16[256,3072]{1,0:T(8,128)(2,1)} %cur_ref.1, bf16[3072]{0:T(1024)(128)(2,1)} %g_kv_ref.1, bf16[2,3072]{1,0:T(2,128)(2,1)} %g_next_ref.3, bf16[3072,3072]{1,0:T(8,128)(2,1)} %wk_ref.1, bf16[3072,3072]{1,0:T(8,128)(2,1)} %wv_ref.1, ...), custom_call_target="tpu_custom_call" | custom-call | flops 14495514624 | bytes 56623104 | tf_op jit(solution)/shard_map/first_project/pallas_call | solution.py:171
  112.4 50.9 %attention.2 = bf16[16,192,256]{2,1,0:T(8,128)(2,1)} custom-call(bf16[16,192,256]{2,1,0:T(8,128)(2,1)} %get-tuple-element.9.q_ref, bf16[2,16,192,256]{3,2,1,0:T(8,128)(2,1)} %get-tuple-element.10.kv_ref), custom_call_target="tpu_custom_call" | custom-call | flops 6442450944 | bytes 6291456 | tf_op jit(solution)/shard_map/attention/pallas_call | solution.py:315
  163.3 106.3 %layer_dense.2 = (bf16[256,3072]{1,0:T(8,128)(2,1)}, bf16[16,192,256]{2,1,0:T(8,128)(2,1)}) custom-call(bf16[3072,256]{1,0:T(8,128)(2,1)} %bitcast.5, bf16[256,3072]{1,0:T(8,128)(2,1)} %cur_ref.1, bf16[2,3072]{1,0:T(2,128)(2,1)} %g_mlp_ref.3, bf16[2,3072]{1,0:T(2,128)(2,1)} %g_next_ref.3, bf16[2,3072,3072]{2,1,0:T(8,128)(2,1)} %bitcast.3, ...), custom_call_target="tpu_custom_call" | custom-call | flops 48318382080 | bytes 188743680 | tf_op jit(solution)/shard_map/layer_dense/pallas_call | solution.py:516
  269.5 52.4 %attention.3 = bf16[16,192,256]{2,1,0:T(8,128)(2,1)} custom-call(bf16[16,192,256]{2,1,0:T(8,128)(2,1)} %get-tuple-element.11.q_ref, bf16[2,16,192,256]{3,2,1,0:T(8,128)(2,1)} %get-tuple-element.10.kv_ref), custom_call_target="tpu_custom_call" | custom-call | flops 6442450944 | bytes 6291456 | tf_op jit(solution)/shard_map/attention/pallas_call | solution.py:315
  321.9 64.6 %layer_dense.3 = bf16[256,3072]{1,0:T(8,128)(2,1)} custom-call(bf16[3072,256]{1,0:T(8,128)(2,1)} %bitcast.6, bf16[256,3072]{1,0:T(8,128)(2,1)} %get-tuple-element.12.cur_ref, bf16[2,3072]{1,0:T(2,128)(2,1)} %g_mlp_ref.3, bf16[2,3072]{1,0:T(2,128)(2,1)} %g_next_ref.3, bf16[2,3072,3072]{2,1,0:T(8,128)(2,1)} %bitcast.4, bf16[2,3072,8192]{2,1,0:T(8,128)(2,1)} %wg_ref.3, ...), custom_call_target="tpu_custom_call" | custom-call | flops 43486543872 | bytes 169869312 | tf_op jit(solution)/shard_map/layer_dense/pallas_call | solution.py:516

commit v5 on v4

--- a/solution.py
+++ b/solution.py
@@ -128,7 +128,7 @@
         for j in range(4):
             send_block(
                 lambda i: buf.at[tensor, i], dst_of(tensor), send_sem.at[tensor], recv_sem.at[tensor],
-                local_sem.at[tensor], 4 * tile_of(t) + lax.rem(me + j, 4), me, cp_size,
+                local_sem.at[tensor], 4 * tile_of(t) + j, me, cp_size,
             )
 
     for t in range(LOOKAHEAD):
@@ -190,7 +190,7 @@
 
 
 def attention_kernel(
-    n, cp_size, head_dim, q_ref, kv_ref, o_ref, k_nat, v_all, s_scr, top_scr, max_scr, sum_scr, acc_scr, buf,
+    n, cp_size, head_dim, q_ref, kv_ref, o_ref, k_nat, v_all, s_even, s_odd, top_even, top_odd, max_scr, sum_scr, acc_scr, buf,
     send_sem, recv_sem, local_sem,
 ):
     me = my_index(cp_size)
@@ -222,9 +222,10 @@
         near = k // side
         return ((1 - mine) * (1 - near) + mine * near) * side + lax.rem(me + k + near, side)
 
-    def scores(k, pair, masked):
+    s_bufs, tops = (s_even, s_odd), (top_even, top_odd)
+
+    def scores(k, pair, masked, slot):
         t = block_of(k)
-        slot = lax.rem(k, 2)
         for h in range(heads):
             q_t = q_ref[t, h * head_dim:(h + 1) * head_dim, :]
             s = jnp.dot(k_nat[h, cols(pair, span), :], q_t, preferred_element_type=F32)
@@ -232,14 +233,13 @@
                 key = lax.broadcasted_iota(jnp.int32, s.shape, 0) + pair * span
                 query = lax.broadcasted_iota(jnp.int32, s.shape, 1) + t * rows
                 s = jnp.where(key <= query, s, NEG_BIG)
-            s_scr[slot, h, cols(pair, span), :] = s
+            s_bufs[slot][h, cols(pair, span), :] = s
             top = jnp.max(s.reshape(span // 8, 8, rows), axis=0)
-            top_scr[slot, h] = jnp.maximum(top_scr[slot, h], top)
-
-    def values(k, pair):
-        slot = lax.rem(k, 2)
+            tops[slot][h] = jnp.maximum(tops[slot][h], top)
+
+    def values(pair, slot):
         for h in range(heads):
-            s = s_scr[slot, h, cols(pair, span), :].reshape(span // 8, 8, rows)
+            s = s_bufs[slot][h, cols(pair, span), :].reshape(span // 8, 8, rows)
             p = jnp.exp2(s * scale - max_scr[h][None])
             sum_scr[h] = sum_scr[h] + jnp.sum(p, axis=0)
             p = p.reshape(span, rows).astype(BF16)
@@ -252,17 +252,12 @@
 
         lax.fori_loop(lo, hi, body, 0)
 
-    def clear_top(k):
-        top_scr[lax.rem(k, 2)] = jnp.full(top_scr.shape[1:], NEG_BIG, F32)
-
-    clear_top(jnp.int32(0))
-    loop(0, block_of(0) // 2, lambda pair: scores(0, pair, False))
-    scores(0, block_of(0) // 2, True)
-    barrier_wait(n)
-
-    def begin_values(k):
+    def clear_top(slot):
+        tops[slot][...] = jnp.full(tops[slot].shape, NEG_BIG, F32)
+
+    def begin_values(slot):
         for h in range(heads):
-            top = jnp.max(top_scr[lax.rem(k, 2), h], axis=0, keepdims=True) * scale
+            top = jnp.max(tops[slot][h], axis=0, keepdims=True) * scale
             max_scr[h] = jnp.broadcast_to(top, max_scr.shape[1:])
         sum_scr[...] = jnp.zeros(sum_scr.shape, F32)
         acc_scr[...] = jnp.zeros(acc_scr.shape, F32)
@@ -275,16 +270,16 @@
     def send(k):
         send_block(src_of, dst_of, send_sem, recv_sem, local_sem, block_of(k), me, cp_size)
 
-    def block(k, carry):
+    def block(k, slot):
         last = block_of(k) // 2
         last_next = block_of(k + 1) // 2
-        begin_values(k)
-        clear_top(k + 1)
+        begin_values(slot)
+        clear_top(1 - slot)
         both = jnp.minimum(last, last_next)
 
         def fused(pair):
-            scores(k + 1, pair, False)
-            values(k, pair)
+            scores(k + 1, pair, False, 1 - slot)
+            values(pair, slot)
 
         loop(0, both, fused)
 
@@ -292,17 +287,31 @@
         def _():
             send(k - 1)
 
-        loop(both, last, lambda pair: values(k, pair))
-        loop(both, last_next, lambda pair: scores(k + 1, pair, False))
-        scores(k + 1, last_next, True)
-        values(k, last)
+        loop(both, last, lambda pair: values(pair, slot))
+        loop(both, last_next, lambda pair: scores(k + 1, pair, False, 1 - slot))
+        scores(k + 1, last_next, True, 1 - slot)
+        values(last, slot)
         end_values(k)
-        return carry
-
-    lax.fori_loop(0, n - 1, block, 0)
-    begin_values(n - 1)
+
+    first = jnp.int32(0)
+    clear_top(0)
+    loop(0, block_of(first) // 2, lambda pair: scores(first, pair, False, 0))
+    scores(first, block_of(first) // 2, True, 0)
+    barrier_wait(n)
+
+    def two_blocks(j, carry):
+        block(2 * j, 0)
+
+        @pl.when(2 * j + 1 < n - 1)
+        def _():
+            block(2 * j + 1, 1)
+
+        return carry
+
+    lax.fori_loop(0, n // 2, two_blocks, 0)
+    begin_values(1)
     send(n - 2)
-    loop(0, me // 2 + 1, lambda pair: values(n - 1, pair))
+    loop(0, me // 2 + 1, lambda pair: values(pair, 1))
     end_values(n - 1)
     send(n - 1)
     finish_blocks(src_of, dst_of, send_sem, recv_sem, local_sem, me, n, cp_size)
@@ -320,8 +329,10 @@
         scratch_shapes=[
             pltpu.VMEM((heads, n * rows, head_dim), BF16),
             pltpu.VMEM((heads, head_dim, n * rows), BF16),
-            pltpu.VMEM((2, heads, n * rows, rows), F32),
-            pltpu.VMEM((2, heads, 8, rows), F32),
+            pltpu.VMEM((heads, n * rows, rows), F32),
+            pltpu.VMEM((heads, n * rows, rows), F32),
+            pltpu.VMEM((heads, 8, rows), F32),
+            pltpu.VMEM((heads, 8, rows), F32),
             pltpu.VMEM((heads, 8, rows), F32),
             pltpu.VMEM((heads, 8, rows), F32),
             pltpu.VMEM((heads, head_dim, rows), F32),
@@ -344,9 +355,9 @@
     n, cp_size, layer, has_next, ot_ref, cur_ref, g_mlp_ref, g_next_ref, wo_ref, wg_ref, wu_ref, wd_ref, wq_ref, *refs
 ):
     if has_next:
-        out_ref, q_ref, mixed, ot_scr, inner, ring, ring_down, sems, in_sems, buf, send_sem, recv_sem, local_sem = refs
+        out_ref, q_ref, mixed, inner, ring, ring_down, sems, buf, send_sem, recv_sem, local_sem = refs
     else:
-        out_ref, mixed, ot_scr, inner, ring, ring_down, sems, in_sems = refs
+        out_ref, mixed, inner, ring, ring_down, sems = refs
     normed = mixed
     rows, width = cur_ref.shape
     hidden = wg_ref.shape[2]
@@ -407,25 +418,18 @@
         pltpu.make_async_copy(wg_ref.at[layer, :, pl.ds(0, COLS)], narrow, sems.at[slot]).wait()
         return narrow[...]
 
-    ot_copy = pltpu.make_async_copy(ot_ref, ot_scr, in_sems.at[0])
-    cur_copy = pltpu.make_async_copy(cur_ref, out_ref, in_sems.at[1])
-    ot_copy.start()
-    start(jnp.int32(0))
-    cur_copy.start()
-    for t in range(1, LOOKAHEAD):
+    for t in range(LOOKAHEAD):
         start(jnp.int32(t))
-    ot_copy.wait()
 
     def flip(i, carry):
-        mixed[:, cols(i, 256)] = ot_scr[cols(i, 256), :].T
+        mixed[:, cols(i, 256)] = ot_ref[cols(i, 256), :].T
         return carry
 
     lax.fori_loop(0, width // 256, flip, 0)
-    cur_copy.wait()
 
     def out_body(t, carry):
         attn = jnp.dot(mixed[...], take_wide(t), preferred_element_type=F32).astype(BF16)
-        out_ref[:, cols(t, WIDE)] = (out_ref[:, cols(t, WIDE)].astype(F32) + attn.astype(F32)).astype(BF16)
+        out_ref[:, cols(t, WIDE)] = (cur_ref[:, cols(t, WIDE)].astype(F32) + attn.astype(F32)).astype(BF16)
         start(t + LOOKAHEAD)
         return carry
 
@@ -467,7 +471,7 @@
 
         def send(i):
             for j in range(4):
-                peer = 4 * tile_of(i) + lax.rem(me + j, 4)
+                peer = 4 * tile_of(i) + j
                 send_block(src_of, dst_of, send_sem, recv_sem, local_sem, peer, me, cp_size)
 
         def q_body(i, carry):
@@ -494,12 +498,10 @@
     out_specs = [vmem]
     scratch = [
         pltpu.VMEM((rows, width), BF16),
-        pltpu.VMEM((width, rows), BF16),
         pltpu.VMEM((rows, hidden), BF16),
         pltpu.VMEM((LOOKAHEAD, width, WIDE), BF16),
         pltpu.VMEM((LOOKAHEAD, hidden, DOWN_COLS), BF16),
         pltpu.SemaphoreType.DMA((LOOKAHEAD,)),
-        pltpu.SemaphoreType.DMA((2,)),
     ]
     params = dict(vmem_limit_bytes=VMEM_LIMIT)
     if has_next:
@@ -515,7 +517,7 @@
     macs = rows * width * ((2 if has_next else 1) * width + 3 * hidden)
     return pl.pallas_call(
         functools.partial(layer_kernel, n, cp_size, layer, has_next),
-        in_specs=[hbm] * 2 + [vmem] * 2 + [hbm] * 5,
+        in_specs=[vmem] * 4 + [hbm] * 5,
         out_specs=out_specs,
         out_shape=out_shape,
         scratch_shapes=scratch,

time: 391 us -> 369 us (0.944)
  Pallas kernels: 387 us -> 366 us
    pallas_call x2, Pallas kernels: 103 us -> 88.1 us  [attention(): pl.pallas_call(functools.partial(attention_kernel, n, cp_size, head_dim),...]
    pallas_call x2, Pallas kernels: 171 us -> 166 us  [layer_dense(): pl.pallas_call(functools.partial(layer_kernel, n, cp_size, layer, has_nex...]
where the time goes in v5:
time: 369 us; the launch traced here: 366 us
  Pallas kernels  366 us (99%)
    pallas_call x2, Pallas kernels, layer_dense(): pl.pallas_call(functools.partial(layer_kernel, n, cp_size, layer, has_nex...  166 us
    pallas_call x1, Pallas kernels, first_project(): pl.pallas_call(functools.partial(first_kernel, n, cp_size), in_specs=[vme...  113 us
    pallas_call x2, Pallas kernels, attention(): pl.pallas_call(functools.partial(attention_kernel, n, cp_size, head_dim),...  88.1 us

profile of v5, /device:TPU:29, one launch (start us, length us, event | category | flops | bytes accessed | tf_op | source)
XLA Modules:
  0.0 366.5 jit_solution(15939298668669624063)
XLA Ops:
  0.0 112.5 %first_project.1 = (bf16[2,16,192,256]{3,2,1,0:T(8,128)(2,1)}, bf16[16,192,256]{2,1,0:T(8,128)(2,1)}) custom-call(bf16[256,3072]{1,0:T(8,128)(2,1)} %cur_ref.1, bf16[3072]{0:T(1024)(128)(2,1)} %g_kv_ref.1, bf16[2,3072]{1,0:T(2,128)(2,1)} %g_next_ref.3, bf16[3072,3072]{1,0:T(8,128)(2,1)} %wk_ref.1, bf16[3072,3072]{1,0:T(8,128)(2,1)} %wv_ref.1, ...), custom_call_target="tpu_custom_call" | custom-call | flops 14495514624 | bytes 56623104 | tf_op jit(solution)/shard_map/first_project/pallas_call | solution.py:171
  112.6 44.2 %attention.2 = bf16[16,192,256]{2,1,0:T(8,128)(2,1)} custom-call(bf16[16,192,256]{2,1,0:T(8,128)(2,1)} %get-tuple-element.9.q_ref, bf16[2,16,192,256]{3,2,1,0:T(8,128)(2,1)} %get-tuple-element.10.kv_ref), custom_call_target="tpu_custom_call" | custom-call | flops 6442450944 | bytes 6291456 | tf_op jit(solution)/shard_map/attention/pallas_call | solution.py:324
  156.8 103.6 %layer_dense.2 = (bf16[256,3072]{1,0:T(8,128)(2,1)}, bf16[16,192,256]{2,1,0:T(8,128)(2,1)}) custom-call(bf16[3072,256]{1,0:T(8,128)(2,1)} %bitcast.5, bf16[256,3072]{1,0:T(8,128)(2,1)} %cur_ref.1, bf16[2,3072]{1,0:T(2,128)(2,1)} %g_mlp_ref.3, bf16[2,3072]{1,0:T(2,128)(2,1)} %g_next_ref.3, bf16[2,3072,3072]{2,1,0:T(8,128)(2,1)} %bitcast.3, ...), custom_call_target="tpu_custom_call" | custom-call | flops 48318382080 | bytes 188743680 | tf_op jit(solution)/shard_map/layer_dense/pallas_call | solution.py:518
  260.4 43.8 %attention.3 = bf16[16,192,256]{2,1,0:T(8,128)(2,1)} custom-call(bf16[16,192,256]{2,1,0:T(8,128)(2,1)} %get-tuple-element.11.q_ref, bf16[2,16,192,256]{3,2,1,0:T(8,128)(2,1)} %get-tuple-element.10.kv_ref), custom_call_target="tpu_custom_call" | custom-call | flops 6442450944 | bytes 6291456 | tf_op jit(solution)/shard_map/attention/pallas_call | solution.py:324
  304.2 62.0 %layer_dense.3 = bf16[256,3072]{1,0:T(8,128)(2,1)} custom-call(bf16[3072,256]{1,0:T(8,128)(2,1)} %bitcast.6, bf16[256,3072]{1,0:T(8,128)(2,1)} %get-tuple-element.12.cur_ref, bf16[2,3072]{1,0:T(2,128)(2,1)} %g_mlp_ref.3, bf16[2,3072]{1,0:T(2,128)(2,1)} %g_next_ref.3, bf16[2,3072,3072]{2,1,0:T(8,128)(2,1)} %bitcast.4, bf16[2,3072,8192]{2,1,0:T(8,128)(2,1)} %wg_ref.3, ...), custom_call_target="tpu_custom_call" | custom-call | flops 43486543872 | bytes 169869312 | tf_op jit(solution)/shard_map/layer_dense/pallas_call | solution.py:518

commit v6 on v5

--- a/solution.py
+++ b/solution.py
@@ -134,10 +134,11 @@
     for t in range(LOOKAHEAD):
         start(jnp.int32(t))
     norm_into(normed, x_ref, g_kv_ref[...].reshape(1, x_ref.shape[1]))
-    norm_into(normed_q, x_ref, g_q_ref[0:1, :])
     barrier_wait(n)
     for tensor in range(3):
         source = normed_q if tensor == 2 else normed
+        if tensor == 2:
+            norm_into(normed_q, x_ref, g_q_ref[0:1, :])
 
         def body(i, carry, tensor=tensor, source=source):
             t = tensor * per + i

time: 369 us -> 369 us (level)
  no operation moved by 1% of the time
where the time goes in v6:
time: 369 us; the launch traced here: 366 us
  Pallas kernels  366 us (99%)
    pallas_call x2, Pallas kernels, layer_dense(): pl.pallas_call(functools.partial(layer_kernel, n, cp_size, layer, has_nex...  166 us
    pallas_call x1, Pallas kernels, first_project(): pl.pallas_call(functools.partial(first_kernel, n, cp_size), in_specs=[vme...  113 us
    pallas_call x2, Pallas kernels, attention(): pl.pallas_call(functools.partial(attention_kernel, n, cp_size, head_dim),...  88 us

profile of v6, /device:TPU:29, one launch (start us, length us, event | category | flops | bytes accessed | tf_op | source)
XLA Modules:
  0.0 366.4 jit_solution(9971694149335023321)
XLA Ops:
  0.0 112.5 %first_project.1 = (bf16[2,16,192,256]{3,2,1,0:T(8,128)(2,1)}, bf16[16,192,256]{2,1,0:T(8,128)(2,1)}) custom-call(bf16[256,3072]{1,0:T(8,128)(2,1)} %cur_ref.1, bf16[3072]{0:T(1024)(128)(2,1)} %g_kv_ref.1, bf16[2,3072]{1,0:T(2,128)(2,1)} %g_next_ref.3, bf16[3072,3072]{1,0:T(8,128)(2,1)} %wk_ref.1, bf16[3072,3072]{1,0:T(8,128)(2,1)} %wv_ref.1, ...), custom_call_target="tpu_custom_call" | custom-call | flops 14495514624 | bytes 56623104 | tf_op jit(solution)/shard_map/first_project/pallas_call | solution.py:172
  112.6 44.2 %attention.2 = bf16[16,192,256]{2,1,0:T(8,128)(2,1)} custom-call(bf16[16,192,256]{2,1,0:T(8,128)(2,1)} %get-tuple-element.9.q_ref, bf16[2,16,192,256]{3,2,1,0:T(8,128)(2,1)} %get-tuple-element.10.kv_ref), custom_call_target="tpu_custom_call" | custom-call | flops 6442450944 | bytes 6291456 | tf_op jit(solution)/shard_map/attention/pallas_call | solution.py:325
  156.8 103.6 %layer_dense.2 = (bf16[256,3072]{1,0:T(8,128)(2,1)}, bf16[16,192,256]{2,1,0:T(8,128)(2,1)}) custom-call(bf16[3072,256]{1,0:T(8,128)(2,1)} %bitcast.5, bf16[256,3072]{1,0:T(8,128)(2,1)} %cur_ref.1, bf16[2,3072]{1,0:T(2,128)(2,1)} %g_mlp_ref.3, bf16[2,3072]{1,0:T(2,128)(2,1)} %g_next_ref.3, bf16[2,3072,3072]{2,1,0:T(8,128)(2,1)} %bitcast.3, ...), custom_call_target="tpu_custom_call" | custom-call | flops 48318382080 | bytes 188743680 | tf_op jit(solution)/shard_map/layer_dense/pallas_call | solution.py:519
  260.4 43.8 %attention.3 = bf16[16,192,256]{2,1,0:T(8,128)(2,1)} custom-call(bf16[16,192,256]{2,1,0:T(8,128)(2,1)} %get-tuple-element.11.q_ref, bf16[2,16,192,256]{3,2,1,0:T(8,128)(2,1)} %get-tuple-element.10.kv_ref), custom_call_target="tpu_custom_call" | custom-call | flops 6442450944 | bytes 6291456 | tf_op jit(solution)/shard_map/attention/pallas_call | solution.py:325
  304.2 62.0 %layer_dense.3 = bf16[256,3072]{1,0:T(8,128)(2,1)} custom-call(bf16[3072,256]{1,0:T(8,128)(2,1)} %bitcast.6, bf16[256,3072]{1,0:T(8,128)(2,1)} %get-tuple-element.12.cur_ref, bf16[2,3072]{1,0:T(2,128)(2,1)} %g_mlp_ref.3, bf16[2,3072]{1,0:T(2,128)(2,1)} %g_next_ref.3, bf16[2,3072,3072]{2,1,0:T(8,128)(2,1)} %bitcast.4, bf16[2,3072,8192]{2,1,0:T(8,128)(2,1)} %wg_ref.3, ...), custom_call_target="tpu_custom_call" | custom-call | flops 43486543872 | bytes 169869312 | tf_op jit(solution)/shard_map/layer_dense/pallas_call | solution.py:519
